TPU v7x, 32 devices: a whole 2x2x4 slice. The times are simulated.
32 devices in a mesh: gx: 2 (over y), gy: 4 (over x, core), gz: 4 (over z).
Axes of the slice: x: 2, y: 2, z: 4, core: 2. Of those that a mesh axis runs over, the one named last changes fastest.
Arguments:
- volume: float32 [16, 64, 512], P(('gx', 'gy'), None, 'gz'), may hold values from 0 to 1
- levels: int32 [4], replicated, may hold values from 0 to 255
Outputs:
- labelling: float32 [4, 16, 64, 512], P(None, 'gx', 'gy', 'gz')
- centers: float32 [4], replicated
All inputs are finite; a program needn't handle non-finite values.
Results may differ from a plain program's by a relative error of at most 0.0001.
Values sent between devices are 32-bit elements; how exact they have to be, the bound alone decides.
No kernel may reach another device: no remote copies, remote signals or barrier semaphores. Data moves between devices by JAX's collectives and lax.ppermute only.
A program may use at most 64 MiB of HBM per device.

v0:
```python
import jax
import jax.numpy as jnp
from jax import lax
from jax.sharding import PartitionSpec as P

ITERS = 2


tau_step = 0.25
sigma_step = 0.25
smooth_weight = 0.5
prior_weight = 1.0


def with_halo(block, sides, width):
    for axis, dim in sides:
        count = lax.axis_size(axis)
        forward = [(i, i + 1) for i in range(count - 1)]
        backward = [(target, source) for source, target in forward]
        low = lax.ppermute(
            lax.slice_in_dim(block, block.shape[dim] - width, None, axis=dim), axis, forward
        )
        high = lax.ppermute(lax.slice_in_dim(block, 0, width, axis=dim), axis, backward)
        block = jnp.concatenate([low, block, high], axis=dim)
    return block


def project_simplex(values):
    how_many = values.shape[0]
    threshold = None
    for subset in range(1, 1 << how_many):
        members = [label_index for label_index in range(how_many) if subset >> label_index & 1]
        summed = values[members[0]]
        for label_index in members[1:]:
            summed = summed + values[label_index]
        candidate = (summed - 1.0) / float(len(members))
        threshold = candidate if threshold is None else jnp.maximum(threshold, candidate)
    return jnp.maximum(values - threshold[None], 0.0)


def bounds(start, total, extent):
    position = start - 1 + jnp.arange(extent + 1, dtype=jnp.int32)
    return (position >= 0, position < total - 1)


def local(volume, levels):
    thickness = volume.shape[0]
    x_start = (lax.axis_index("gx") * lax.axis_size("gy") + lax.axis_index("gy")) * thickness
    x_total = thickness * lax.axis_size("gx") * lax.axis_size("gy")
    y_start = 0
    y_total = volume.shape[1]
    z_start = lax.axis_index("gz") * volume.shape[2]
    z_total = volume.shape[2] * lax.axis_size("gz")
    extent = volume.shape
    how_many = levels.shape[0]
    inside_x, ahead_x = bounds(x_start, x_total, extent[0])
    inside_y, ahead_y = bounds(y_start, y_total, extent[1])
    inside_z, ahead_z = bounds(z_start, z_total, extent[2])
    inside = (inside_x[:, None, None] & inside_y[None, :, None] & inside_z[None, None, :]).astype(
        jnp.float32
    )
    base_levels = levels.astype(jnp.float32) / 255.0
    centers = base_levels
    starting = (volume[None] - base_levels[:, None, None, None]) ** 2
    labelling = project_simplex(1.0 / how_many - tau_step * starting)
    smoothed = labelling
    dual_field = jnp.zeros((how_many, 3, extent[0] + 1, extent[1] + 1, extent[2] + 1), jnp.float32)
    for iteration in range(ITERS):
        padded = with_halo(smoothed, ((("gx", "gy"), 1), ("gz", 3)), 1)
        padded = jnp.pad(padded, ((0, 0), (0, 0), (1, 1), (0, 0)))
        corner = padded[:, :-1, :-1, :-1]
        grad_x = jnp.where(ahead_x[:, None, None], padded[:, 1:, :-1, :-1] - corner, 0.0)
        grad_y = jnp.where(ahead_y[None, :, None], padded[:, :-1, 1:, :-1] - corner, 0.0)
        grad_z = jnp.where(ahead_z[None, None, :], padded[:, :-1, :-1, 1:] - corner, 0.0)
        stepped = dual_field + sigma_step * jnp.stack([grad_x, grad_y, grad_z], axis=1)
        length = jnp.sqrt(
            stepped[:, 0] * stepped[:, 0]
            + stepped[:, 1] * stepped[:, 1]
            + stepped[:, 2] * stepped[:, 2]
        )
        shrink = inside / jnp.maximum(1.0, length / smooth_weight)
        dual_field = stepped * shrink[:, None]
        divergence = (
            dual_field[:, 0, 1:, 1:, 1:]
            - dual_field[:, 0, :-1, 1:, 1:]
            + (dual_field[:, 1, 1:, 1:, 1:] - dual_field[:, 1, 1:, :-1, 1:])
            + (dual_field[:, 2, 1:, 1:, 1:] - dual_field[:, 2, 1:, 1:, :-1])
        )
        fidelity = (volume[None] - centers[:, None, None, None]) ** 2
        updated = project_simplex(labelling + tau_step * (divergence - fidelity))
        smoothed = 2.0 * updated - labelling
        labelling = updated
        sizes_local = jnp.sum(labelling, axis=(1, 2, 3))
        weighted = jnp.sum(labelling * volume[None], axis=(1, 2, 3))
        sizes_all, weighted_all = lax.psum((sizes_local, weighted), ("gx", "gy", "gz"))
        centers = (weighted_all + prior_weight * base_levels) / (sizes_all + prior_weight)
    labelling = lax.all_to_all(labelling, "gy", split_axis=2, concat_axis=1, tiled=True)
    return (labelling, centers)


def solution(mesh):
    return jax.shard_map(
        local,
        mesh=mesh,
        in_specs=(P(("gx", "gy"), None, "gz"), P()),
        out_specs=(P(None, "gx", "gy", "gz"), P()),
        check_vma=False,
    )
```

profile of v0, /device:TPU:0, one launch (start us, length us, event | category | flops | bytes accessed | tf_op | source)
XLA Modules:
  0.0 159.2 jit_solution(3588290688517704985)
XLA Ops:
  0.6 0.7 convert_multiply_fusion
  1.3 0.9 multiply_subtract_fusion.1
  2.4 0.6 copy-done.8
  3.0 1.0 subtract_maximum_fusion.2
  4.0 2.4 %collective-permute-start = (f32[4,1,64,128]{3,2,1,0:T(8,128)S(1)}, f32[4,1,64,128]{3,2,1,0:T(8,128)S(1)}, u32[]{:S(2)}, u32[]{:S(2)}) collective-permute-start(f32[4,1,64,128]{3,2,1,0:T(8,128)S(1)} %get-tuple-element.24), channel_id=1, source_target_pairs={{0,4},{4,8},{8,12},{12,16},{16,20},{20,24},{24,28},{1,5},{5,9},{9,... | collective-permute-start | bytes 393224 | tf_op jit(solution)/shard_map/ppermute | solution.py:20
  6.4 1.3 collective-permute-start.1
  8.0 3.7 %collective-permute-done.1 = f32[4,1,64,128]{3,2,1,0:T(8,128)S(1)} collective-permute-done((f32[4,1,64,128]{3,2,1,0:T(8,128)S(1)}, f32[4,1,64,128]{3,2,1,0:T(8,128)S(1)}, u32[]{:S(2)}, u32[]{:S(2)}) %collective-permute-start.1) | collective-permute-done | bytes 131104 | tf_op jit(solution)/shard_map/ppermute | solution.py:23
  12.0 3.5 %collective-permute-start.2 = (f32[4,4,64,1]{3,2,1,0:T(8,128)S(1)}, f32[4,4,64,1]{3,2,1,0:T(8,128)S(1)}, u32[]{:S(2)}, u32[]{:S(2)}) collective-permute-start(f32[4,4,64,1]{3,2,1,0:T(8,128)S(1)} %get-tuple-element.19), channel_id=1, source_target_pairs={{0,1},{1,2},{2,3},{4,5},{5,6},{6,7},{8,9},{9,10},{10,11},{12,13},{... | collective-permute-start | bytes 12296 | tf_op jit(solution)/shard_map/ppermute | solution.py:20
  15.5 1.3 collective-permute-start.3
  16.8 8.4 %collective-permute-done.2 = f32[4,4,64,1]{3,2,1,0:T(8,128)S(1)} collective-permute-done((f32[4,4,64,1]{3,2,1,0:T(8,128)S(1)}, f32[4,4,64,1]{3,2,1,0:T(8,128)S(1)}, u32[]{:S(2)}, u32[]{:S(2)}) %collective-permute-start.2) | collective-permute-done | bytes 4128 | tf_op jit(solution)/shard_map/ppermute | solution.py:20
  25.2 4.7 %collective-permute-done.3 = f32[4,4,64,1]{3,2,1,0:T(8,128)S(1)} collective-permute-done((f32[4,4,64,1]{3,2,1,0:T(8,128)S(1)}, f32[4,4,64,1]{3,2,1,0:T(8,128)S(1)}, u32[]{:S(2)}, u32[]{:S(2)}) %collective-permute-start.3) | collective-permute-done | bytes 4128 | tf_op jit(solution)/shard_map/ppermute | solution.py:23
  29.9 0.5 select_maximum_fusion.4
  33.1 0.9 copy-done
  34.1 1.1 multiply_reduce_fusion.1
  35.2 0.7 copy-done.2
  35.9 0.7 fusion.67
  36.6 4.7 %collective-permute-start.4 = (f32[4,1,64,128]{3,2,1,0:T(8,128)}, f32[4,1,64,128]{3,2,1,0:T(8,128)}, u32[]{:S(2)}, u32[]{:S(2)}) collective-permute-start(f32[4,1,64,128]{3,2,1,0:T(8,128)} %get-tuple-element.22), channel_id=1, source_target_pairs={{0,4},{4,8},{8,12},{12,16},{16,20},{20,24},{24,28},{1,5},{5,9},{9,... | collective-permute-start | bytes 393224 | tf_op jit(solution)/shard_map/ppermute | solution.py:20
  41.3 1.3 collective-permute-start.5
  42.6 44.4 %all-reduce.3 = (f32[4]{0:T(128)}, f32[4]{0:T(128)}) all-reduce(f32[4]{0:T(128)} %get-tuple-element.3, f32[4]{0:T(128)} %get-tuple-element.2), channel_id=1, replica_groups=mesh['gx'=2,'gy'=4,'gz'=4] {'gx','gy','gz'}, use_global_device_ids=true, to_apply=%region_3.4 | all-reduce | flops 8 | bytes 64 | tf_op jit(solution)/shard_map/psum | solution.py:95
  87.0 1.1 pad_maximum_fusion.2
  88.4 2.3 %collective-permute-start.6 = (f32[4,4,64,1]{3,2,1,0:T(8,128)S(1)}, f32[4,4,64,1]{3,2,1,0:T(8,128)S(1)}, u32[]{:S(2)}, u32[]{:S(2)}) collective-permute-start(f32[4,4,64,1]{3,2,1,0:T(8,128)S(1)} %get-tuple-element.17), channel_id=1, source_target_pairs={{0,1},{1,2},{2,3},{4,5},{5,6},{6,7},{8,9},{9,10},{10,11},{12,13},{... | collective-permute-start | bytes 12296 | tf_op jit(solution)/shard_map/ppermute | solution.py:20
  90.7 1.3 collective-permute-start.7
  92.1 9.2 %collective-permute-done.6 = f32[4,4,64,1]{3,2,1,0:T(8,128)S(1)} collective-permute-done((f32[4,4,64,1]{3,2,1,0:T(8,128)S(1)}, f32[4,4,64,1]{3,2,1,0:T(8,128)S(1)}, u32[]{:S(2)}, u32[]{:S(2)}) %collective-permute-start.6) | collective-permute-done | bytes 4128 | tf_op jit(solution)/shard_map/ppermute | solution.py:20
  101.3 4.1 %collective-permute-done.7 = f32[4,4,64,1]{3,2,1,0:T(8,128)S(1)} collective-permute-done((f32[4,4,64,1]{3,2,1,0:T(8,128)S(1)}, f32[4,4,64,1]{3,2,1,0:T(8,128)S(1)}, u32[]{:S(2)}, u32[]{:S(2)}) %collective-permute-start.7) | collective-permute-done | bytes 4128 | tf_op jit(solution)/shard_map/ppermute | solution.py:23
  105.5 1.5 select_maximum_fusion
  109.4 1.2 copy-done.1
  110.6 0.8 fusion.35
  111.6 0.9 copy.8
  112.5 3.9 %all-to-all-start = ((f32[4,2,64,128]{3,1,0,2:T(2,128)}), f32[4,2,64,128]{3,1,0,2:T(2,128)S(1)}, u32[]{:S(2)}, u32[]{:S(2)}) async-start(f32[4,2,64,128]{3,1,0,2:T(2,128)} %copy.8), calls=%async_computation | async-start | bytes 524288 | tf_op jit(solution)/shard_map/all_to_all | solution.py:97
  116.4 41.5 %all-reduce.2 = (f32[4]{0:T(128)S(1)}, f32[4]{0:T(128)S(1)}) all-reduce(f32[4]{0:T(128)S(1)} %get-tuple-element.5, f32[4]{0:T(128)S(1)} %get-tuple-element.4), channel_id=1, replica_groups=mesh['gx'=2,'gy'=4,'gz'=4] {'gx','gy','gz'}, use_global_device_ids=true, to_apply=%region_7.8 | all-reduce | flops 8 | bytes 64 | tf_op jit(solution)/shard_map/psum | solution.py:95
  157.9 0.5 add_divide_fusion
  158.5 0.7 copy.10
  (63 shorter events, 6.2 us)
Async XLA Ops:
  2.4 0.6 copy-start.8
  4.0 4.0 %collective-permute-start = (f32[4,1,64,128]{3,2,1,0:T(8,128)S(1)}, f32[4,1,64,128]{3,2,1,0:T(8,128)S(1)}, u32[]{:S(2)}, u32[]{:S(2)}) collective-permute-start(f32[4,1,64,128]{3,2,1,0:T(8,128)S(1)} %get-tuple-element.24), channel_id=1, source_target_pairs={{0,4},{4,8},{8,12},{12,16},{16,20},{20,24},{24,28},{1,5},{5,9},{9,... | collective-permute-start | bytes 393224 | tf_op jit(solution)/shard_map/ppermute | solution.py:20
  6.4 5.3 %collective-permute-start.1 = (f32[4,1,64,128]{3,2,1,0:T(8,128)S(1)}, f32[4,1,64,128]{3,2,1,0:T(8,128)S(1)}, u32[]{:S(2)}, u32[]{:S(2)}) collective-permute-start(f32[4,1,64,128]{3,2,1,0:T(8,128)S(1)} %get-tuple-element.25), channel_id=1, source_target_pairs={{4,0},{8,4},{12,8},{16,12},{20,16},{24,20},{28,24},{5,1},{9,5},{13... | collective-permute-start | bytes 393224 | tf_op jit(solution)/shard_map/ppermute | solution.py:23
  7.9 23.2 %copy-start.6 = (f32[3,65,129]{2,1,0:T(8,128)}, f32[3,65,129]{2,1,0:T(8,128)S(1)}, u32[]{:S(2)}) copy-start(f32[3,65,129]{2,1,0:T(8,128)S(1)} %and_convert_fusion) | copy-start | bytes 301864
  12.0 13.2 %collective-permute-start.2 = (f32[4,4,64,1]{3,2,1,0:T(8,128)S(1)}, f32[4,4,64,1]{3,2,1,0:T(8,128)S(1)}, u32[]{:S(2)}, u32[]{:S(2)}) collective-permute-start(f32[4,4,64,1]{3,2,1,0:T(8,128)S(1)} %get-tuple-element.19), channel_id=1, source_target_pairs={{0,1},{1,2},{2,3},{4,5},{5,6},{6,7},{8,9},{9,10},{10,11},{12,13},{... | collective-permute-start | bytes 12296 | tf_op jit(solution)/shard_map/ppermute | solution.py:20
  15.5 14.4 %collective-permute-start.3 = (f32[4,4,64,1]{3,2,1,0:T(8,128)S(1)}, f32[4,4,64,1]{3,2,1,0:T(8,128)S(1)}, u32[]{:S(2)}, u32[]{:S(2)}) collective-permute-start(f32[4,4,64,1]{3,2,1,0:T(8,128)S(1)} %get-tuple-element.20), channel_id=1, source_target_pairs={{1,0},{2,1},{3,2},{5,4},{6,5},{7,6},{9,8},{10,9},{11,10},{13,12},{... | collective-permute-start | bytes 12296 | tf_op jit(solution)/shard_map/ppermute | solution.py:23
  16.8 14.1 %copy-start.14 = (pred[65]{0:T(512)(128)(4,1)}, pred[65]{0:T(512)(128)(4,1)S(1)}, u32[]{:S(2)}) copy-start(pred[65]{0:T(512)(128)(4,1)S(1)} %fusion.62) | copy-start | bytes 199
  31.7 0.8 copy-start.4
  31.7 0.9 copy-start.9
  32.5 1.5 copy-start
  34.1 2.6 %copy-start.11 = (f32[2,64,128]{2,1,0:T(8,128)}, f32[2,64,128]{2,1,0:T(8,128)S(1)}, u32[]{:S(2)}) copy-start(f32[2,64,128]{2,1,0:T(8,128)S(1)} %maximum_bitcast_fusion.1) | copy-start | bytes 196612
  34.1 58.0 %copy-start.13 = (s32[4]{0:T(128)S(1)}, s32[4]{0:T(128)}, u32[]{:S(2)}) copy-start(s32[4]{0:T(128)} %param.3) | copy-start | bytes 52
  35.2 0.7 copy-start.2
  36.6 50.4 %collective-permute-start.4 = (f32[4,1,64,128]{3,2,1,0:T(8,128)}, f32[4,1,64,128]{3,2,1,0:T(8,128)}, u32[]{:S(2)}, u32[]{:S(2)}) collective-permute-start(f32[4,1,64,128]{3,2,1,0:T(8,128)} %get-tuple-element.22), channel_id=1, source_target_pairs={{0,4},{4,8},{8,12},{12,16},{16,20},{20,24},{24,28},{1,5},{5,9},{9,... | collective-permute-start | bytes 393224 | tf_op jit(solution)/shard_map/ppermute | solution.py:20
  41.3 45.7 %collective-permute-start.5 = (f32[4,1,64,128]{3,2,1,0:T(8,128)}, f32[4,1,64,128]{3,2,1,0:T(8,128)}, u32[]{:S(2)}, u32[]{:S(2)}) collective-permute-start(f32[4,1,64,128]{3,2,1,0:T(8,128)} %get-tuple-element.23), channel_id=1, source_target_pairs={{4,0},{8,4},{12,8},{16,12},{20,16},{24,20},{28,24},{5,1},{9,5},{13... | collective-permute-start | bytes 393224 | tf_op jit(solution)/shard_map/ppermute | solution.py:23
  87.0 5.0 %copy-start.16 = (f32[4]{0:T(128)S(1)}, f32[4]{0:T(128)}, u32[]{:S(2)}) copy-start(f32[4]{0:T(128)} %get-tuple-element.8) | copy-start | bytes 52
  87.0 5.0 %copy-start.17 = (f32[4]{0:T(128)S(1)}, f32[4]{0:T(128)}, u32[]{:S(2)}) copy-start(f32[4]{0:T(128)} %get-tuple-element.9) | copy-start | bytes 52
  87.0 18.4 %copy-start.3 = (f32[4,2,64,128]{3,2,1,0:T(8,128)S(1)}, f32[4,2,64,128]{3,2,1,0:T(8,128)}, u32[]{:S(2)}) copy-start(f32[4,2,64,128]{3,2,1,0:T(8,128)} %copy-done.2) | copy-start | bytes 786436
  88.2 18.8 %copy-start.15 = (pred[65]{0:T(512)(128)(4,1)S(1)}, pred[65]{0:T(512)(128)(4,1)}, u32[]{:S(2)}) copy-start(pred[65]{0:T(512)(128)(4,1)} %copy-done.14) | copy-start | bytes 199
  88.4 12.9 %collective-permute-start.6 = (f32[4,4,64,1]{3,2,1,0:T(8,128)S(1)}, f32[4,4,64,1]{3,2,1,0:T(8,128)S(1)}, u32[]{:S(2)}, u32[]{:S(2)}) collective-permute-start(f32[4,4,64,1]{3,2,1,0:T(8,128)S(1)} %get-tuple-element.17), channel_id=1, source_target_pairs={{0,1},{1,2},{2,3},{4,5},{5,6},{6,7},{8,9},{9,10},{10,11},{12,13},{... | collective-permute-start | bytes 12296 | tf_op jit(solution)/shard_map/ppermute | solution.py:20
  90.7 14.7 %collective-permute-start.7 = (f32[4,4,64,1]{3,2,1,0:T(8,128)S(1)}, f32[4,4,64,1]{3,2,1,0:T(8,128)S(1)}, u32[]{:S(2)}, u32[]{:S(2)}) collective-permute-start(f32[4,4,64,1]{3,2,1,0:T(8,128)S(1)} %get-tuple-element.18), channel_id=1, source_target_pairs={{1,0},{2,1},{3,2},{5,4},{6,5},{7,6},{9,8},{10,9},{11,10},{13,12},{... | collective-permute-start | bytes 12296 | tf_op jit(solution)/shard_map/ppermute | solution.py:23
  107.4 0.9 copy-start.7
  108.8 1.8 %copy-start.1 = (f32[4,3,3,65,129]{4,3,2,0,1:T(8,128)S(1)}, f32[4,3,3,65,129]{4,3,2,0,1:T(8,128)}, u32[]{:S(2)}) copy-start(f32[4,3,3,65,129]{4,3,2,0,1:T(8,128)} %copy-done) | copy-start | bytes 3622324
  108.8 1.7 %copy-start.5 = (f32[2,64,128]{2,1,0:T(8,128)S(1)}, f32[2,64,128]{2,1,0:T(8,128)}, u32[]{:S(2)}) copy-start(f32[2,64,128]{2,1,0:T(8,128)} %param.2) | copy-start | bytes 196612
  108.8 1.7 %copy-start.10 = (f32[2,64,128]{2,1,0:T(8,128)S(1)}, f32[2,64,128]{2,1,0:T(8,128)}, u32[]{:S(2)}) copy-start(f32[2,64,128]{2,1,0:T(8,128)} %copy-done.8) | copy-start | bytes 196612
  108.8 1.7 %copy-start.12 = (f32[2,64,128]{2,1,0:T(8,128)S(1)}, f32[2,64,128]{2,1,0:T(8,128)}, u32[]{:S(2)}) copy-start(f32[2,64,128]{2,1,0:T(8,128)} %copy-done.11) | copy-start | bytes 196612
  112.5 45.9 %all-to-all-start = ((f32[4,2,64,128]{3,1,0,2:T(2,128)}), f32[4,2,64,128]{3,1,0,2:T(2,128)S(1)}, u32[]{:S(2)}, u32[]{:S(2)}) async-start(f32[4,2,64,128]{3,1,0,2:T(2,128)} %copy.8), calls=%async_computation | async-start | bytes 524288 | tf_op jit(solution)/shard_map/all_to_all | solution.py:97
where the time goes:
time: 160 us; the launch traced here: 159 us
  blocking collectives  85.9 us (54%)
  waiting for transfers between devices  30.2 us (19%)
  starting transfers between devices  22 us (14%)
  other arithmetic  12.8 us (8%)
  local copies, waits for them, and re-layouts  7.36 us (5%)
    psum x2, blocking collectives, local(): lax.psum((sizes_local, weighted), ('gx', 'gy', 'gz'))  85.9 us
    ppermute x4, waiting for transfers between devices, with_halo(): lax.ppermute(lax.slice_in_dim(block, block.shape[dim] - width, None, axis...  17.6 us
    ppermute x4, starting transfers between devices, with_halo(): lax.ppermute(lax.slice_in_dim(block, block.shape[dim] - width, None, axis...  12.9 us
    ppermute x4, waiting for transfers between devices, with_halo(): lax.ppermute(lax.slice_in_dim(block, 0, width, axis=dim), axis, backward)  12.6 us
    ppermute x4, starting transfers between devices, with_halo(): lax.ppermute(lax.slice_in_dim(block, 0, width, axis=dim), axis, backward)  5.16 us
    unnamed x36, local copies, waits for them, and re-layouts  4.51 us
    all_to_all x1, starting transfers between devices, local(): lax.all_to_all(labelling, 'gy', split_axis=2, concat_axis=1, tiled=True)  3.9 us
  transfers between devices with their start and end apart: 9, of which 5 were waited for; matrix products, arithmetic and copies ran while one was open for 0% of the time, Pallas kernels for 0%

commit v1 on v0

--- a/solution.py
+++ b/solution.py
@@ -36,6 +36,15 @@
         candidate = (summed - 1.0) / float(len(members))
         threshold = candidate if threshold is None else jnp.maximum(threshold, candidate)
     return jnp.maximum(values - threshold[None], 0.0)
+
+
+def sum_over_devices(partial):
+    axes = ("gx", "gy", "gz")
+    devices = lax.axis_size(axes)
+    flat = jnp.pad(partial.reshape(1, 1, -1), ((0, 0), (0, 0), (0, 128 - partial.size)))
+    spread = jnp.broadcast_to(flat, (devices, 1, 128))
+    total = lax.all_to_all(spread, axes, 0, 0, tiled=True).sum((0, 1))
+    return total[: partial.size].reshape(partial.shape)
 
 
 def bounds(start, total, extent):
@@ -92,7 +101,7 @@
         labelling = updated
         sizes_local = jnp.sum(labelling, axis=(1, 2, 3))
         weighted = jnp.sum(labelling * volume[None], axis=(1, 2, 3))
-        sizes_all, weighted_all = lax.psum((sizes_local, weighted), ("gx", "gy", "gz"))
+        sizes_all, weighted_all = sum_over_devices(jnp.stack([sizes_local, weighted]))
         centers = (weighted_all + prior_weight * base_levels) / (sizes_all + prior_weight)
     labelling = lax.all_to_all(labelling, "gy", split_axis=2, concat_axis=1, tiled=True)
     return (labelling, centers)

time: 160 us -> 106 us (0.66)
  blocking collectives: 85.9 us -> 16 us
  waiting for transfers between devices: 30.2 us -> 42.4 us
  starting transfers between devices: 22 us -> 24.1 us
    psum x2 -> x0, blocking collectives: 85.9 us -> none  [local(): lax.psum((sizes_local, weighted), ('gx', 'gy', 'gz'))]
    all_to_all x0 -> x1, blocking collectives: none -> 16 us  [sum_over_devices(): total = lax.all_to_all(spread, axes, 0, 0, tiled=True).sum((0, 1))]
    all_to_all x0 -> x1, waiting for transfers between devices: none -> 6.29 us  [sum_over_devices(): total = lax.all_to_all(spread, axes, 0, 0, tiled=True).sum((0, 1))]
    all_to_all x1, waiting for transfers between devices: 0.01 us -> 5.36 us  [local(): lax.all_to_all(labelling, 'gy', split_axis=2, concat_axis=1, tiled=True)]
    all_to_all x0 -> x1, starting transfers between devices: none -> 2.49 us  [sum_over_devices(): total = lax.all_to_all(spread, axes, 0, 0, tiled=True).sum((0, 1))]
    unnamed x36 -> x44, local copies, waits for them, and re-layouts: 4.51 us -> 3.88 us
  transfers between devices with their start and end apart: 9 -> 10, of which waited for: 5 -> 7; matrix products, arithmetic and copies ran while one was open for 0% -> 2% of each run, Pallas kernels for 0% -> 0%
where the time goes in v1:
time: 106 us
  waiting for transfers between devices  42.4 us (40%)
  starting transfers between devices  24.1 us (23%)
  blocking collectives  16 us (15%)
  other arithmetic  13.5 us (13%)
  local copies, waits for them, and re-layouts  8.51 us (8%)
  between operations  1.14 us (1%)
    ppermute x4, waiting for transfers between devices, with_halo(): lax.ppermute(lax.slice_in_dim(block, block.shape[dim] - width, None, axis...  18.2 us
    all_to_all x1, blocking collectives, sum_over_devices(): total = lax.all_to_all(spread, axes, 0, 0, tiled=True).sum((0, 1))  16 us
    ppermute x4, starting transfers between devices, with_halo(): lax.ppermute(lax.slice_in_dim(block, block.shape[dim] - width, None, axis...  13 us
    ppermute x4, waiting for transfers between devices, with_halo(): lax.ppermute(lax.slice_in_dim(block, 0, width, axis=dim), axis, backward)  12.6 us
    all_to_all x1, waiting for transfers between devices, sum_over_devices(): total = lax.all_to_all(spread, axes, 0, 0, tiled=True).sum((0, 1))  6.29 us
    all_to_all x1, waiting for transfers between devices, local(): lax.all_to_all(labelling, 'gy', split_axis=2, concat_axis=1, tiled=True)  5.36 us
    ppermute x4, starting transfers between devices, with_halo(): lax.ppermute(lax.slice_in_dim(block, 0, width, axis=dim), axis, backward)  5.16 us
    unnamed x44, local copies, waits for them, and re-layouts  3.88 us
  transfers between devices with their start and end apart: 10, of which 7 were waited for; matrix products, arithmetic and copies ran while one was open for 2% of the time, Pallas kernels for 0%

profile of v1, /device:TPU:0, one launch (start us, length us, event | category | flops | bytes accessed | tf_op | source)
XLA Modules:
  0.0 105.5 jit_solution(12309736381671861654)
XLA Ops:
  0.6 0.7 convert_multiply_fusion
  1.3 0.9 multiply_subtract_fusion.1
  2.4 0.6 copy-done.7
  3.0 1.0 subtract_maximum_fusion.2
  4.0 2.4 %collective-permute-start = (f32[4,1,64,128]{3,2,1,0:T(8,128)S(1)}, f32[4,1,64,128]{3,2,1,0:T(8,128)S(1)}, u32[]{:S(2)}, u32[]{:S(2)}) collective-permute-start(f32[4,1,64,128]{3,2,1,0:T(8,128)S(1)} %get-tuple-element.20), channel_id=1, source_target_pairs={{0,4},{4,8},{8,12},{12,16},{16,20},{20,24},{24,28},{1,5},{5,9},{9,... | collective-permute-start | bytes 393224 | tf_op jit(solution)/shard_map/ppermute | solution.py:20
  6.4 1.3 %collective-permute-start.1 = (f32[4,1,64,128]{3,2,1,0:T(8,128)S(1)}, f32[4,1,64,128]{3,2,1,0:T(8,128)S(1)}, u32[]{:S(2)}, u32[]{:S(2)}) collective-permute-start(f32[4,1,64,128]{3,2,1,0:T(8,128)S(1)} %get-tuple-element.21), channel_id=1, source_target_pairs={{4,0},{8,4},{12,8},{16,12},{20,16},{24,20},{28,24},{5,1},{9,5},{13... | collective-permute-start | bytes 393224 | tf_op jit(solution)/shard_map/ppermute | solution.py:23
  8.0 3.7 %collective-permute-done.1 = f32[4,1,64,128]{3,2,1,0:T(8,128)S(1)} collective-permute-done((f32[4,1,64,128]{3,2,1,0:T(8,128)S(1)}, f32[4,1,64,128]{3,2,1,0:T(8,128)S(1)}, u32[]{:S(2)}, u32[]{:S(2)}) %collective-permute-start.1) | collective-permute-done | bytes 131104 | tf_op jit(solution)/shard_map/ppermute | solution.py:23
  12.0 3.5 %collective-permute-start.2 = (f32[4,4,64,1]{3,2,1,0:T(8,128)S(1)}, f32[4,4,64,1]{3,2,1,0:T(8,128)S(1)}, u32[]{:S(2)}, u32[]{:S(2)}) collective-permute-start(f32[4,4,64,1]{3,2,1,0:T(8,128)S(1)} %get-tuple-element.15), channel_id=1, source_target_pairs={{0,1},{1,2},{2,3},{4,5},{5,6},{6,7},{8,9},{9,10},{10,11},{12,13},{... | collective-permute-start | bytes 12296 | tf_op jit(solution)/shard_map/ppermute | solution.py:20
  15.5 1.3 %collective-permute-start.3 = (f32[4,4,64,1]{3,2,1,0:T(8,128)S(1)}, f32[4,4,64,1]{3,2,1,0:T(8,128)S(1)}, u32[]{:S(2)}, u32[]{:S(2)}) collective-permute-start(f32[4,4,64,1]{3,2,1,0:T(8,128)S(1)} %get-tuple-element.16), channel_id=1, source_target_pairs={{1,0},{2,1},{3,2},{5,4},{6,5},{7,6},{9,8},{10,9},{11,10},{13,12},{... | collective-permute-start | bytes 12296 | tf_op jit(solution)/shard_map/ppermute | solution.py:23
  16.8 8.4 %collective-permute-done.2 = f32[4,4,64,1]{3,2,1,0:T(8,128)S(1)} collective-permute-done((f32[4,4,64,1]{3,2,1,0:T(8,128)S(1)}, f32[4,4,64,1]{3,2,1,0:T(8,128)S(1)}, u32[]{:S(2)}, u32[]{:S(2)}) %collective-permute-start.2) | collective-permute-done | bytes 4128 | tf_op jit(solution)/shard_map/ppermute | solution.py:20
  25.2 4.7 %collective-permute-done.3 = f32[4,4,64,1]{3,2,1,0:T(8,128)S(1)} collective-permute-done((f32[4,4,64,1]{3,2,1,0:T(8,128)S(1)}, f32[4,4,64,1]{3,2,1,0:T(8,128)S(1)}, u32[]{:S(2)}, u32[]{:S(2)}) %collective-permute-start.3) | collective-permute-done | bytes 4128 | tf_op jit(solution)/shard_map/ppermute | solution.py:23
  33.2 0.9 copy-done
  34.1 1.2 %fusion.43 = (f32[4]{0:T(128)S(1)}, f32[4]{0:T(128)S(1)}, f32[4,2,64,128]{3,2,1,0:T(8,128)}) fusion(f32[2,64,128]{2,1,0:T(8,128)S(1)} %maximum_bitcast_fusion.1, f32[2,64,128]{2,1,0:T(8,128)S(1)} %copy-done.3, f32[2,64,128]{2,1,0:T(8,128)S(1)} %copy-done.8, f32[4]{0:T(128)S(1)} %convert_multiply_fusion, f32[4,3,3,65,129]{4,3,2,0,1:T(8,128)S(1)} %fusion.1), kind=kLoop, calls=%fused_computation.85 | loop fusion | flops 1376248 | bytes 2031664 | tf_op jit(solution)/shard_map/reduce_sum | solution.py:102
  35.4 1.7 %fusion.68 = (f32[4,1,64,128]{3,2,1,0:T(8,128)}, f32[4,1,64,128]{3,2,1,0:T(8,128)}) fusion(f32[4,2,64,128]{3,2,1,0:T(8,128)} %get-tuple-element.17), kind=kLoop, calls=%fused_computation.127 | loop fusion | bytes 524288 | tf_op jit(solution)/shard_map/slice | solution.py:21
  37.1 4.7 %collective-permute-start.4 = (f32[4,1,64,128]{3,2,1,0:T(8,128)}, f32[4,1,64,128]{3,2,1,0:T(8,128)}, u32[]{:S(2)}, u32[]{:S(2)}) collective-permute-start(f32[4,1,64,128]{3,2,1,0:T(8,128)} %get-tuple-element.18), channel_id=1, source_target_pairs={{0,4},{4,8},{8,12},{12,16},{16,20},{20,24},{24,28},{1,5},{5,9},{9,... | collective-permute-start | bytes 393224 | tf_op jit(solution)/shard_map/ppermute | solution.py:20
  41.7 1.3 %collective-permute-start.5 = (f32[4,1,64,128]{3,2,1,0:T(8,128)}, f32[4,1,64,128]{3,2,1,0:T(8,128)}, u32[]{:S(2)}, u32[]{:S(2)}) collective-permute-start(f32[4,1,64,128]{3,2,1,0:T(8,128)} %get-tuple-element.19), channel_id=1, source_target_pairs={{4,0},{8,4},{12,8},{16,12},{20,16},{24,20},{28,24},{5,1},{9,5},{13... | collective-permute-start | bytes 393224 | tf_op jit(solution)/shard_map/ppermute | solution.py:23
  43.1 16.0 %all_to_all.28 = f32[32,1,128]{2,1,0:T(1,128)S(1)} all-to-all(f32[32,1,128]{2,1,0:T(1,128)S(1)} %broadcast_in_dim.89), channel_id=1, replica_groups=mesh['gx'=2,'gy'=4,'gz'=4] {'gx','gy','gz'}, dimensions={0} | all-to-all | bytes 32768 | tf_op jit(solution)/shard_map/all_to_all | solution.py:46
  59.6 1.1 %pad_maximum_fusion.2 = f32[4,4,64,128]{3,2,1,0:T(8,128)S(1)} fusion(f32[4,1,64,128]{3,2,1,0:T(8,128)} %collective-permute-done.5, f32[4,2,64,128]{3,2,1,0:T(8,128)} %get-tuple-element.17, f32[4,1,64,128]{3,2,1,0:T(8,128)} %collective-permute-done.4), kind=kLoop, calls=%fused_computation.57 | loop fusion | flops 262144 | bytes 1048576 | tf_op jit(solution)/shard_map/concatenate | solution.py:24
  61.0 2.4 %collective-permute-start.6 = (f32[4,4,64,1]{3,2,1,0:T(8,128)S(1)}, f32[4,4,64,1]{3,2,1,0:T(8,128)S(1)}, u32[]{:S(2)}, u32[]{:S(2)}) collective-permute-start(f32[4,4,64,1]{3,2,1,0:T(8,128)S(1)} %get-tuple-element.13), channel_id=1, source_target_pairs={{0,1},{1,2},{2,3},{4,5},{5,6},{6,7},{8,9},{9,10},{10,11},{12,13},{... | collective-permute-start | bytes 12296 | tf_op jit(solution)/shard_map/ppermute | solution.py:20
  63.4 1.3 %collective-permute-start.7 = (f32[4,4,64,1]{3,2,1,0:T(8,128)S(1)}, f32[4,4,64,1]{3,2,1,0:T(8,128)S(1)}, u32[]{:S(2)}, u32[]{:S(2)}) collective-permute-start(f32[4,4,64,1]{3,2,1,0:T(8,128)S(1)} %get-tuple-element.14), channel_id=1, source_target_pairs={{1,0},{2,1},{3,2},{5,4},{6,5},{7,6},{9,8},{10,9},{11,10},{13,12},{... | collective-permute-start | bytes 12296 | tf_op jit(solution)/shard_map/ppermute | solution.py:23
  64.8 9.8 %collective-permute-done.6 = f32[4,4,64,1]{3,2,1,0:T(8,128)S(1)} collective-permute-done((f32[4,4,64,1]{3,2,1,0:T(8,128)S(1)}, f32[4,4,64,1]{3,2,1,0:T(8,128)S(1)}, u32[]{:S(2)}, u32[]{:S(2)}) %collective-permute-start.6) | collective-permute-done | bytes 4128 | tf_op jit(solution)/shard_map/ppermute | solution.py:20
  74.6 4.1 %collective-permute-done.7 = f32[4,4,64,1]{3,2,1,0:T(8,128)S(1)} collective-permute-done((f32[4,4,64,1]{3,2,1,0:T(8,128)S(1)}, f32[4,4,64,1]{3,2,1,0:T(8,128)S(1)}, u32[]{:S(2)}, u32[]{:S(2)}) %collective-permute-start.7) | collective-permute-done | bytes 4128 | tf_op jit(solution)/shard_map/ppermute | solution.py:23
  78.7 1.5 %select_maximum_fusion = f32[4,4,66,130]{3,2,1,0:T(8,128)S(1)} fusion(f32[4,4,64,1]{3,2,1,0:T(8,128)S(1)} %collective-permute-done.7, f32[4,4,64,1]{3,2,1,0:T(8,128)S(1)} %collective-permute-done.6, f32[4,1,64,128]{3,2,1,0:T(8,128)} %collective-permute-done.5, f32[4,2,64,128]{3,2,1,0:T(8,128)S(1)} %copy-done.2, f32[4,1,64,128]{3,2,1,0:T(8,128)} %collective-permute-done.4), kind=kLoop, calls=%fused_computation.8 | loop fusion | flops 1647360 | bytes 1081600 | tf_op jit(solution)/shard_map/concatenate | solution.py:24
  82.7 1.2 %copy-done.1 = f32[4,3,3,65,129]{4,3,2,0,1:T(8,128)S(1)} copy-done((f32[4,3,3,65,129]{4,3,2,0,1:T(8,128)S(1)}, f32[4,3,3,65,129]{4,3,2,0,1:T(8,128)}, u32[]{:S(2)}) %copy-start.1) | copy-done | bytes 1207464
  83.9 0.8 fusion.35
  85.1 0.6 broadcast_in_dim.91
  85.7 2.5 %all-to-all-start.2 = ((f32[32,1,128]{2,1,0:T(1,128)}), f32[32,1,128]{2,1,0:T(1,128)S(1)}, u32[]{:S(2)}, u32[]{:S(2)}) async-start(f32[32,1,128]{2,1,0:T(1,128)} %broadcast_in_dim.91), calls=%async_computation.2 | async-start | bytes 32768 | tf_op jit(solution)/shard_map/all_to_all | solution.py:46
  88.2 0.9 copy.17
  89.1 6.3 %all-to-all-done.2 = f32[32,1,128]{2,1,0:T(1,128)S(1)} async-done(((f32[32,1,128]{2,1,0:T(1,128)}), f32[32,1,128]{2,1,0:T(1,128)S(1)}, u32[]{:S(2)}, u32[]{:S(2)}) %all-to-all-start.2) | async-done | bytes 16416 | tf_op jit(solution)/shard_map/all_to_all | solution.py:46
  95.4 3.4 %all-to-all-start.1 = ((f32[4,2,64,128]{3,1,0,2:T(2,128)}), f32[4,2,64,128]{3,1,0,2:T(2,128)S(1)}, u32[]{:S(2)}, u32[]{:S(2)}) async-start(f32[4,2,64,128]{3,1,0,2:T(2,128)} %copy.17), calls=%async_computation.1 | async-start | bytes 524288 | tf_op jit(solution)/shard_map/all_to_all | solution.py:106
  99.4 5.4 %all-to-all-done.1 = f32[4,2,64,128]{3,1,0,2:T(2,128)S(1)} async-done(((f32[4,2,64,128]{3,1,0,2:T(2,128)}), f32[4,2,64,128]{3,1,0,2:T(2,128)S(1)}, u32[]{:S(2)}, u32[]{:S(2)}) %all-to-all-start.1) | async-done | bytes 262176 | tf_op jit(solution)/shard_map/all_to_all | solution.py:106
  104.8 0.7 copy.19
  (82 shorter events, 8.2 us)
Async XLA Ops:
  1.3 31.9 %copy-start.12 = (f32[4]{0:T(128)}, f32[4]{0:T(128)S(1)}, u32[]{:S(2)}) copy-start(f32[4]{0:T(128)S(1)} %convert_multiply_fusion) | copy-start | bytes 52
  2.4 0.6 copy-start.7
  4.0 4.0 %collective-permute-start = (f32[4,1,64,128]{3,2,1,0:T(8,128)S(1)}, f32[4,1,64,128]{3,2,1,0:T(8,128)S(1)}, u32[]{:S(2)}, u32[]{:S(2)}) collective-permute-start(f32[4,1,64,128]{3,2,1,0:T(8,128)S(1)} %get-tuple-element.20), channel_id=1, source_target_pairs={{0,4},{4,8},{8,12},{12,16},{16,20},{20,24},{24,28},{1,5},{5,9},{9,... | collective-permute-start | bytes 393224 | tf_op jit(solution)/shard_map/ppermute | solution.py:20
  6.4 5.3 %collective-permute-start.1 = (f32[4,1,64,128]{3,2,1,0:T(8,128)S(1)}, f32[4,1,64,128]{3,2,1,0:T(8,128)S(1)}, u32[]{:S(2)}, u32[]{:S(2)}) collective-permute-start(f32[4,1,64,128]{3,2,1,0:T(8,128)S(1)} %get-tuple-element.21), channel_id=1, source_target_pairs={{4,0},{8,4},{12,8},{16,12},{20,16},{24,20},{28,24},{5,1},{9,5},{13... | collective-permute-start | bytes 393224 | tf_op jit(solution)/shard_map/ppermute | solution.py:23
  7.9 23.3 %copy-start.5 = (f32[3,65,129]{2,1,0:T(8,128)}, f32[3,65,129]{2,1,0:T(8,128)S(1)}, u32[]{:S(2)}) copy-start(f32[3,65,129]{2,1,0:T(8,128)S(1)} %and_convert_fusion) | copy-start | bytes 301864
  7.9 22.5 %copy-start.16 = (pred[3]{0:T(512)(128)(4,1)}, pred[3]{0:T(512)(128)(4,1)S(1)}, u32[]{:S(2)}) copy-start(pred[3]{0:T(512)(128)(4,1)S(1)} %fusion.64) | copy-start | bytes 13
  8.0 22.5 %copy-start.18 = (pred[129]{0:T(512)(128)(4,1)}, pred[129]{0:T(512)(128)(4,1)S(1)}, u32[]{:S(2)}) copy-start(pred[129]{0:T(512)(128)(4,1)S(1)} %fusion.60) | copy-start | bytes 391
  12.0 13.2 %collective-permute-start.2 = (f32[4,4,64,1]{3,2,1,0:T(8,128)S(1)}, f32[4,4,64,1]{3,2,1,0:T(8,128)S(1)}, u32[]{:S(2)}, u32[]{:S(2)}) collective-permute-start(f32[4,4,64,1]{3,2,1,0:T(8,128)S(1)} %get-tuple-element.15), channel_id=1, source_target_pairs={{0,1},{1,2},{2,3},{4,5},{5,6},{6,7},{8,9},{9,10},{10,11},{12,13},{... | collective-permute-start | bytes 12296 | tf_op jit(solution)/shard_map/ppermute | solution.py:20
  15.5 14.4 %collective-permute-start.3 = (f32[4,4,64,1]{3,2,1,0:T(8,128)S(1)}, f32[4,4,64,1]{3,2,1,0:T(8,128)S(1)}, u32[]{:S(2)}, u32[]{:S(2)}) collective-permute-start(f32[4,4,64,1]{3,2,1,0:T(8,128)S(1)} %get-tuple-element.16), channel_id=1, source_target_pairs={{1,0},{2,1},{3,2},{5,4},{6,5},{7,6},{9,8},{10,9},{11,10},{13,12},{... | collective-permute-start | bytes 12296 | tf_op jit(solution)/shard_map/ppermute | solution.py:23
  16.8 14.1 %copy-start.20 = (pred[65]{0:T(512)(128)(4,1)}, pred[65]{0:T(512)(128)(4,1)S(1)}, u32[]{:S(2)}) copy-start(pred[65]{0:T(512)(128)(4,1)S(1)} %fusion.62) | copy-start | bytes 199
  31.7 0.8 copy-start.3
  31.7 0.9 copy-start.8
  32.6 1.5 %copy-start = (f32[4,3,3,65,129]{4,3,2,0,1:T(8,128)}, f32[4,3,3,65,129]{4,3,2,0,1:T(8,128)S(1)}, u32[]{:S(2)}) copy-start(f32[4,3,3,65,129]{4,3,2,0,1:T(8,128)S(1)} %fusion.1) | copy-start | bytes 3622324
  34.1 1.2 %copy-start.10 = (f32[2,64,128]{2,1,0:T(8,128)}, f32[2,64,128]{2,1,0:T(8,128)S(1)}, u32[]{:S(2)}) copy-start(f32[2,64,128]{2,1,0:T(8,128)S(1)} %maximum_bitcast_fusion.1) | copy-start | bytes 196612
  37.1 22.5 %collective-permute-start.4 = (f32[4,1,64,128]{3,2,1,0:T(8,128)}, f32[4,1,64,128]{3,2,1,0:T(8,128)}, u32[]{:S(2)}, u32[]{:S(2)}) collective-permute-start(f32[4,1,64,128]{3,2,1,0:T(8,128)} %get-tuple-element.18), channel_id=1, source_target_pairs={{0,4},{4,8},{8,12},{12,16},{16,20},{20,24},{24,28},{1,5},{5,9},{9,... | collective-permute-start | bytes 393224 | tf_op jit(solution)/shard_map/ppermute | solution.py:20
  41.7 17.8 %collective-permute-start.5 = (f32[4,1,64,128]{3,2,1,0:T(8,128)}, f32[4,1,64,128]{3,2,1,0:T(8,128)}, u32[]{:S(2)}, u32[]{:S(2)}) collective-permute-start(f32[4,1,64,128]{3,2,1,0:T(8,128)} %get-tuple-element.19), channel_id=1, source_target_pairs={{4,0},{8,4},{12,8},{16,12},{20,16},{24,20},{28,24},{5,1},{9,5},{13... | collective-permute-start | bytes 393224 | tf_op jit(solution)/shard_map/ppermute | solution.py:23
  59.6 5.1 %copy-start.14 = (f32[128]{0:T(128)S(1)}, f32[128]{0:T(128)}, u32[]{:S(2)}) copy-start(f32[128]{0:T(128)} %reduce_sum.56) | copy-start | bytes 1540
  59.6 5.1 %copy-start.15 = (s32[4]{0:T(128)S(1)}, s32[4]{0:T(128)}, u32[]{:S(2)}) copy-start(s32[4]{0:T(128)} %param.3) | copy-start | bytes 52
  59.6 19.2 %copy-start.2 = (f32[4,2,64,128]{3,2,1,0:T(8,128)S(1)}, f32[4,2,64,128]{3,2,1,0:T(8,128)}, u32[]{:S(2)}) copy-start(f32[4,2,64,128]{3,2,1,0:T(8,128)} %get-tuple-element.17) | copy-start | bytes 786436
  60.7 19.5 %copy-start.17 = (pred[3]{0:T(512)(128)(4,1)S(1)}, pred[3]{0:T(512)(128)(4,1)}, u32[]{:S(2)}) copy-start(pred[3]{0:T(512)(128)(4,1)} %copy-done.16) | copy-start | bytes 13
  60.7 19.5 %copy-start.19 = (pred[129]{0:T(512)(128)(4,1)S(1)}, pred[129]{0:T(512)(128)(4,1)}, u32[]{:S(2)}) copy-start(pred[129]{0:T(512)(128)(4,1)} %copy-done.18) | copy-start | bytes 391
  60.7 19.5 %copy-start.21 = (pred[65]{0:T(512)(128)(4,1)S(1)}, pred[65]{0:T(512)(128)(4,1)}, u32[]{:S(2)}) copy-start(pred[65]{0:T(512)(128)(4,1)} %copy-done.20) | copy-start | bytes 199
  61.0 13.6 %collective-permute-start.6 = (f32[4,4,64,1]{3,2,1,0:T(8,128)S(1)}, f32[4,4,64,1]{3,2,1,0:T(8,128)S(1)}, u32[]{:S(2)}, u32[]{:S(2)}) collective-permute-start(f32[4,4,64,1]{3,2,1,0:T(8,128)S(1)} %get-tuple-element.13), channel_id=1, source_target_pairs={{0,1},{1,2},{2,3},{4,5},{5,6},{6,7},{8,9},{9,10},{10,11},{12,13},{... | collective-permute-start | bytes 12296 | tf_op jit(solution)/shard_map/ppermute | solution.py:20
  63.4 15.3 %collective-permute-start.7 = (f32[4,4,64,1]{3,2,1,0:T(8,128)S(1)}, f32[4,4,64,1]{3,2,1,0:T(8,128)S(1)}, u32[]{:S(2)}, u32[]{:S(2)}) collective-permute-start(f32[4,4,64,1]{3,2,1,0:T(8,128)S(1)} %get-tuple-element.14), channel_id=1, source_target_pairs={{1,0},{2,1},{3,2},{5,4},{6,5},{7,6},{9,8},{10,9},{11,10},{13,12},{... | collective-permute-start | bytes 12296 | tf_op jit(solution)/shard_map/ppermute | solution.py:23
  80.7 0.9 copy-start.6
  82.1 1.8 %copy-start.1 = (f32[4,3,3,65,129]{4,3,2,0,1:T(8,128)S(1)}, f32[4,3,3,65,129]{4,3,2,0,1:T(8,128)}, u32[]{:S(2)}) copy-start(f32[4,3,3,65,129]{4,3,2,0,1:T(8,128)} %copy-done) | copy-start | bytes 3622324
  82.1 1.7 %copy-start.4 = (f32[2,64,128]{2,1,0:T(8,128)S(1)}, f32[2,64,128]{2,1,0:T(8,128)}, u32[]{:S(2)}) copy-start(f32[2,64,128]{2,1,0:T(8,128)} %param.2) | copy-start | bytes 196612
  82.1 1.7 %copy-start.9 = (f32[2,64,128]{2,1,0:T(8,128)S(1)}, f32[2,64,128]{2,1,0:T(8,128)}, u32[]{:S(2)}) copy-start(f32[2,64,128]{2,1,0:T(8,128)} %copy-done.7) | copy-start | bytes 196612
  82.2 1.7 %copy-start.11 = (f32[2,64,128]{2,1,0:T(8,128)S(1)}, f32[2,64,128]{2,1,0:T(8,128)}, u32[]{:S(2)}) copy-start(f32[2,64,128]{2,1,0:T(8,128)} %copy-done.10) | copy-start | bytes 196612
  82.2 1.7 %copy-start.13 = (f32[4]{0:T(128)S(1)}, f32[4]{0:T(128)}, u32[]{:S(2)}) copy-start(f32[4]{0:T(128)} %copy-done.12) | copy-start | bytes 52
  85.7 9.7 %all-to-all-start.2 = ((f32[32,1,128]{2,1,0:T(1,128)}), f32[32,1,128]{2,1,0:T(1,128)S(1)}, u32[]{:S(2)}, u32[]{:S(2)}) async-start(f32[32,1,128]{2,1,0:T(1,128)} %broadcast_in_dim.91), calls=%async_computation.2 | async-start | bytes 32768 | tf_op jit(solution)/shard_map/all_to_all | solution.py:46
  95.4 9.4 %all-to-all-start.1 = ((f32[4,2,64,128]{3,1,0,2:T(2,128)}), f32[4,2,64,128]{3,1,0,2:T(2,128)S(1)}, u32[]{:S(2)}, u32[]{:S(2)}) async-start(f32[4,2,64,128]{3,1,0,2:T(2,128)} %copy.17), calls=%async_computation.1 | async-start | bytes 524288 | tf_op jit(solution)/shard_map/all_to_all | solution.py:106

commit v2 on v0

v2 whole, which is shorter than its diff:
```python
import functools

import jax
import jax.numpy as jnp
from jax import lax
from jax.experimental import pallas as pl
from jax.experimental.pallas import tpu as pltpu
from jax.sharding import PartitionSpec as P

tau_step = 0.25
sigma_step = 0.25
smooth_weight = 0.5
prior_weight = 1.0

AXES = ("gx", "gy", "gz")
SLABS = ("gx", "gy")
ROWS = 5


def project_simplex(values):
    a, b, c, d = values
    a, b = jnp.maximum(a, b), jnp.minimum(a, b)
    c, d = jnp.maximum(c, d), jnp.minimum(c, d)
    a, c = jnp.maximum(a, c), jnp.minimum(a, c)
    b, d = jnp.maximum(b, d), jnp.minimum(b, d)
    b, c = jnp.maximum(b, c), jnp.minimum(b, c)
    one = a - 1.0
    two = one + b
    three = two + c
    four = three + d
    threshold = jnp.maximum(
        jnp.maximum(one, two * 0.5), jnp.maximum(three * (1.0 / 3.0), four * 0.25)
    )
    return [jnp.maximum(value - threshold, 0.0) for value in values]


def fidelities(volume, centers):
    result = []
    for center in centers:
        apart = volume - center
        result.append(tau_step * (apart * apart))
    return result


def first_labels(volume, base):
    return project_simplex([1.0 / len(base) - value for value in fidelities(volume, base)])


def clip_dual(x, y, z):
    square = x * x + y * y + z * z
    shrink = smooth_weight * lax.rsqrt(jnp.maximum(square, smooth_weight * smooth_weight))
    return x * shrink, y * shrink, z * shrink


class Slab:
    def __init__(self, shape):
        self.shape = shape
        self.y = lax.broadcasted_iota(jnp.int32, shape, 0)
        self.z = lax.broadcasted_iota(jnp.int32, shape, 1)

    def ahead(self, value):
        rows, lanes = self.shape
        y = jnp.where(self.y == rows - 1, 0.0, pltpu.roll(value, rows - 1, 0) - value)
        z = jnp.where(self.z == lanes - 1, 0.0, pltpu.roll(value, lanes - 1, 1) - value)
        return y, z

    def behind(self, y, z):
        before_y = jnp.where(self.y == 0, 0.0, pltpu.roll(y, 1, 0))
        before_z = jnp.where(self.z == 0, 0.0, pltpu.roll(z, 1, 1))
        return (y - before_y) + (z - before_z)


class Planes:
    def __init__(self, shape, height, x_first, x_total):
        self.height = height
        self.lanes = shape[1]
        lane = lax.broadcasted_iota(jnp.int32, shape, 1)
        self.low = lane < height
        self.y = jnp.where(self.low, lane, lane - height)
        self.x = x_first + jnp.where(self.low, 0, 1)
        self.last_x = self.x == x_total - 1
        self.first_x = self.x == 0
        self.inside = (self.x >= 0).astype(jnp.float32)
        self.rows = shape[0]

    def ahead_xy(self, value):
        swapped = pltpu.roll(value, self.height, 1)
        following = jnp.where(self.low, swapped, pltpu.roll(swapped, self.rows - 1, 0))
        x = jnp.where(self.last_x, 0.0, following - value)
        y = jnp.where(
            self.y == self.height - 1, 0.0, pltpu.roll(value, self.lanes - 1, 1) - value
        )
        return x, y

    def behind_xy(self, x, y):
        swapped = pltpu.roll(x, self.height, 1)
        before_x = jnp.where(self.low, pltpu.roll(swapped, 1, 0), swapped)
        before_x = jnp.where(self.first_x, 0.0, before_x)
        before_y = jnp.where(self.y == 0, 0.0, pltpu.roll(y, 1, 1))
        return (x - before_x) + (y - before_y)

    def dual(self, value, next_z, old=None):
        x, y = self.ahead_xy(value)
        z = next_z - value
        x, y, z = (sigma_step * component for component in (x, y, z))
        if old is not None:
            x, y, z = (was + component for was, component in zip(old, (x, y, z)))
        return clip_dual(x, y, z)


def total_of(value):
    return jnp.sum(jnp.sum(value, axis=0, keepdims=True), axis=1, keepdims=True)


def rows_of_base(base_ref):
    return [base_ref[label : label + 1, :] for label in range(base_ref.shape[0])]


def pack_sums(sums, shape):
    lane = lax.broadcasted_iota(jnp.int32, shape, 1)
    row = jnp.zeros(shape, jnp.float32)
    for index, value in enumerate(sums):
        row = jnp.where(lane == index, value, row)
    return row


def slab_index():
    return lax.axis_index("gx") * lax.axis_size("gy") + lax.axis_index("gy")


def neighbours(pair_ref, other_ref, layer, low):
    odd = lax.rem(slab_index(), 2) == 1
    if low:
        return jnp.where(odd, pair_ref[layer], other_ref[layer])
    return jnp.where(odd, other_ref[layer], pair_ref[layer])


def first_kernel(v_ref, pair_ref, other_ref, base_ref, out_ref, lab_ref, dual_ref):
    slabs = lax.axis_size(SLABS)
    blocks = lax.axis_size("gz")
    slab, block = slab_index(), lax.axis_index("gz")
    thick, height, depth = v_ref.shape
    labels = base_ref.shape[0]
    base = rows_of_base(base_ref)
    grid = Slab((height, depth))

    volume = [neighbours(pair_ref, other_ref, thick - 1, True)]
    volume += [v_ref[layer] for layer in range(thick)]
    volume += [neighbours(pair_ref, other_ref, 0, False)]
    for layer, values in enumerate(volume):
        for label, value in enumerate(first_labels(values, base)):
            lab_ref[label, layer] = value
    inside = (slab > 0).astype(jnp.float32)
    open_end = sigma_step * (slab < slabs - 1).astype(jnp.float32)
    for label in range(labels):
        for layer in range(thick + 1):
            value = lab_ref[label, layer]
            x = lab_ref[label, layer + 1] - value
            x = x * (open_end if layer == thick else sigma_step)
            y, z = grid.ahead(value)
            x, y, z = clip_dual(x, sigma_step * y, sigma_step * z)
            if layer == 0:
                dual_ref[label, 0, 0] = x * inside
            else:
                dual_ref[label, 0, layer] = x
                dual_ref[label, 1, layer] = grid.behind(y, z)
    first = jnp.where(block > 0, 0, -1)
    last = jnp.where(block < blocks - 1, depth - 1, depth)
    keep = (grid.z != first) & (grid.z != last)
    sums = [None] * (2 * labels)
    for layer in range(thick):
        values = volume[layer + 1]
        away = fidelities(values, base)
        entries = []
        for label in range(labels):
            divergence = (
                dual_ref[label, 0, layer + 1]
                - dual_ref[label, 0, layer]
                + dual_ref[label, 1, layer + 1]
            )
            entries.append(lab_ref[label, layer + 1] + tau_step * divergence - away[label])
        for label, value in enumerate(project_simplex(entries)):
            value = jnp.where(keep, value, 0.0)
            for index, term in ((label, value), (labels + label, value * values)):
                sums[index] = term if sums[index] is None else sums[index] + term
    devices = slabs * blocks
    turned = jnp.transpose(v_ref[...].reshape(thick * height, depth))
    for row, plane in enumerate((0, 1, depth - 2, depth - 1)):
        out_ref[pl.ds(row, devices, stride=ROWS), :] = jnp.broadcast_to(
            turned[plane : plane + 1], (devices, thick * height)
        )
    packed = pack_sums([total_of(value) for value in sums], (1, thick * height))
    out_ref[pl.ds(ROWS - 1, devices, stride=ROWS), :] = jnp.broadcast_to(
        packed, (devices, thick * height)
    )


def ahead_kernel(
    v_ref, pair_ref, other_ref, base_ref, w_ref, q_ref, lab_ref, dual_ref, smooth_ref
):
    slabs = lax.axis_size(SLABS)
    slab = slab_index()
    thick, height, depth = v_ref.shape
    labels = base_ref.shape[0]
    base = rows_of_base(base_ref)
    grid = Slab((height, depth))
    halo = thick
    layers = thick + 2 * halo

    def layer_of(index):
        if index < halo:
            return neighbours(pair_ref, other_ref, index, True)
        if index < halo + thick:
            return v_ref[index - halo]
        return neighbours(pair_ref, other_ref, index - halo - thick, False)

    for layer in range(layers):
        for label, value in enumerate(first_labels(layer_of(layer), base)):
            lab_ref[label, layer] = value
    inside = (slab > 0).astype(jnp.float32)
    open_end = sigma_step * (slab < slabs - 1).astype(jnp.float32)
    end = halo + thick - 1
    for label in range(labels):
        for layer in range(layers - 1):
            value = lab_ref[label, layer]
            x = lab_ref[label, layer + 1] - value
            x = x * (open_end if layer == end else sigma_step)
            y, z = grid.ahead(value)
            x, y, z = clip_dual(x, sigma_step * y, sigma_step * z)
            dual_ref[label, 0, layer] = x * inside if layer == halo - 1 else x
            dual_ref[label, 1, layer] = y
            dual_ref[label, 2, layer] = z
    for layer in range(1, layers - 1):
        away = fidelities(layer_of(layer), base)
        entries = []
        for label in range(labels):
            divergence = (
                dual_ref[label, 0, layer]
                - dual_ref[label, 0, layer - 1]
                + grid.behind(dual_ref[label, 1, layer], dual_ref[label, 2, layer])
            )
            entries.append(lab_ref[label, layer] + tau_step * divergence - away[label])
        for label, value in enumerate(project_simplex(entries)):
            smooth_ref[label, layer] = 2.0 * value - lab_ref[label, layer]
            lab_ref[label, layer] = value
    for label in range(labels):
        before = None
        for layer in range(halo - 1, halo + thick):
            value = smooth_ref[label, layer]
            x = smooth_ref[label, layer + 1] - value
            x = x * (open_end if layer == end else sigma_step)
            y, z = grid.ahead(value)
            x, y, z = clip_dual(
                dual_ref[label, 0, layer] + x,
                dual_ref[label, 1, layer] + sigma_step * y,
                dual_ref[label, 2, layer] + sigma_step * z,
            )
            if layer == halo - 1:
                x = x * inside
            else:
                divergence = (x - before) + grid.behind(y, z)
                w_ref[label, layer - halo] = lab_ref[label, layer] + tau_step * divergence
            before = x
    row = lax.broadcasted_iota(jnp.int32, (8, thick * height), 0)
    near, far = [], []
    for start in (0, halo, halo + thick):
        flat = jnp.concatenate([layer_of(start + index) for index in range(thick)], axis=0)
        turned = jnp.transpose(flat)
        near.append(turned[0:8])
        far.append(turned[depth - 8 : depth])
    for column in range(6):
        plane = jnp.zeros((8, thick * height), jnp.float32)
        for which in range(3):
            if column >= 2:
                source = near[which][column - 2 : column - 1]
                plane = jnp.where(row == which, source, plane)
            if column < 4:
                source = far[which][4 + column : 5 + column]
                plane = jnp.where(row == 4 + which, source, plane)
        q_ref[column] = plane


def last_kernel(
    v_ref, w_ref, q_ref, base_ref, got_ref, sums_ref, *rest
):
    slabs = lax.axis_size(SLABS)
    blocks = lax.axis_size("gz")
    count = lax.axis_size("gy")
    slab, block = slab_index(), lax.axis_index("gz")
    pieces, lab_ref = rest[:count], rest[count]
    thick, height, depth = v_ref.shape
    lanes = thick * height
    labels = base_ref.shape[0]
    base = rows_of_base(base_ref)
    devices = slabs * blocks
    x_total = slabs * thick

    row = lax.broadcasted_iota(jnp.int32, (slabs, lanes), 0)
    everywhere = Planes((slabs, lanes), height, thick * row, x_total)
    sums = [jnp.zeros((slabs, lanes), jnp.float32) for _ in range(2 * labels)]
    for end in range(blocks - 1):
        planes = [
            got_ref[pl.ds((end + beyond) * ROWS + which, slabs, stride=blocks * ROWS), :]
            for beyond, which in ((0, 2), (0, 3), (1, 0), (1, 1))
        ]
        first = [first_labels(plane, base) for plane in planes]
        divergence = [[], []]
        for label in range(labels):
            duals = [
                everywhere.dual(first[index][label], first[index + 1][label])
                for index in range(3)
            ]
            for index in (1, 2):
                x, y, z = duals[index]
                divergence[index - 1].append(
                    everywhere.behind_xy(x, y) + (z - duals[index - 1][2])
                )
        for index in (1, 2):
            away = fidelities(planes[index], base)
            entries = [
                first[index][label] + tau_step * divergence[index - 1][label] - away[label]
                for label in range(labels)
            ]
            for label, value in enumerate(project_simplex(entries)):
                sums[label] = sums[label] + value
                sums[labels + label] = sums[labels + label] + value * planes[index]
    parts = got_ref[pl.ds(ROWS - 1, devices, stride=ROWS), :]
    lane = lax.broadcasted_iota(jnp.int32, (1, lanes), 1)
    parts = jnp.sum(parts, axis=0, keepdims=True)
    for index, value in enumerate(sums):
        parts = parts + jnp.where(lane == index, total_of(value), 0.0)
    whole = [
        jnp.sum(jnp.where(lane == index, parts, 0.0), axis=1, keepdims=True)
        for index in range(2 * labels)
    ]
    centers = [
        (whole[labels + label] + prior_weight * base[label]) / (whole[label] + prior_weight)
        for label in range(labels)
    ]

    row = lax.broadcasted_iota(jnp.int32, (8, lanes), 0)
    local = Planes((8, lanes), height, thick * (slab - 1 + (row & 3)), x_total)
    planes = [q_ref[column] for column in range(6)]
    for which in range(3):
        index = jnp.clip(slab - 1 + which, 0, slabs - 1) * blocks
        low = (index + jnp.maximum(block - 1, 0)) * ROWS
        high = (index + jnp.minimum(block + 1, blocks - 1)) * ROWS
        for column in range(2):
            source = got_ref[pl.ds(low + 2 + column, 1), :]
            planes[column] = jnp.where(row == which, source, planes[column])
            source = got_ref[pl.ds(high + column, 1), :]
            planes[4 + column] = jnp.where(row == 4 + which, source, planes[4 + column])
    first = [first_labels(plane, base) for plane in planes]
    duals = []
    for label in range(labels):
        duals.append([])
        for column in range(5):
            x, y, z = local.dual(first[column][label], first[column + 1][label])
            duals[label].append((x * local.inside, y, z))
    second, smooth = {}, {}
    for column in range(1, 5):
        away = fidelities(planes[column], base)
        entries = []
        for label in range(labels):
            x, y, z = duals[label][column]
            divergence = local.behind_xy(x, y) + (z - duals[label][column - 1][2])
            entries.append(first[column][label] + tau_step * divergence - away[label])
        second[column] = project_simplex(entries)
        smooth[column] = [
            2.0 * second[column][label] - first[column][label] for label in range(labels)
        ]
    for label in range(labels):
        for column in range(1, 4):
            x, y, z = local.dual(
                smooth[column][label], smooth[column + 1][label], duals[label][column]
            )
            duals[label][column] = (x * local.inside, y, z)
    edge = {}
    for column in (2, 3):
        away = fidelities(planes[column], centers)
        entries = []
        for label in range(labels):
            x, y, z = duals[label][column]
            divergence = local.behind_xy(x, y) + (z - duals[label][column - 1][2])
            entries.append(second[column][label] + tau_step * divergence - away[label])
        edge[column] = project_simplex(entries)
    step = depth // labels
    tiles = [jnp.zeros((8, lanes), jnp.float32) for _ in range(depth // 8)]
    for label in range(labels):
        two, three = edge[2][label], edge[3][label]
        tiles[label * step // 8] = tiles[label * step // 8] + jnp.where(
            row == 0, pltpu.roll(two, 7, 0), jnp.where(row == 1, three, 0.0)
        )
        place = (label * step // 8 - 1) % (depth // 8)
        tiles[place] = tiles[place] + jnp.where(
            row == 6, pltpu.roll(two, 1, 0), jnp.where(row == 7, pltpu.roll(three, 2, 0), 0.0)
        )
    columns = jnp.transpose(jnp.concatenate(tiles, axis=0))

    z = lax.broadcasted_iota(jnp.int32, (height, depth), 1)
    replaced = ((z < 2) & (block > 0)) | ((z >= depth - 2) & (block < blocks - 1))
    sums = [None] * (2 * labels)
    for layer in range(thick):
        values = v_ref[layer]
        away = fidelities(values, centers)
        entries = [w_ref[label, layer] - away[label] for label in range(labels)]
        for label, value in enumerate(project_simplex(entries)):
            column = columns[layer * height : (layer + 1) * height]
            if label:
                column = pltpu.roll(column, depth - label * step, 1)
            value = jnp.where(replaced, column, value)
            lab_ref[label, layer] = value
            for index, term in ((label, value), (labels + label, value * values)):
                sums[index] = term if sums[index] is None else sums[index] + term
    packed = pack_sums([total_of(value) for value in sums], (1, lanes))
    sums_ref[...] = jnp.broadcast_to(packed, (devices, lanes))
    rows = height // count
    me = lax.axis_index("gy")
    for other in range(count):
        start = pl.multiple_of((me ^ other) * rows, rows)
        pieces[other][...] = lab_ref[:, :, pl.ds(start, rows), :]


def join_kernel(*refs):
    *pieces, out_ref = refs
    me = lax.axis_index("gy")
    thick = pieces[0].shape[1]
    for other, piece in enumerate(pieces):
        out_ref[:, pl.ds((me ^ other) * thick, thick)] = piece[...]


def local(volume, levels):
    slabs = lax.axis_size(SLABS)
    blocks = lax.axis_size("gz")
    count = lax.axis_size("gy")
    devices = slabs * blocks
    thick, height, depth = volume.shape
    labels = levels.shape[0]
    lanes = thick * height
    if thick != 2 or labels != 4 or count & (count - 1):
        raise ValueError("unsupported sizes")
    f32 = functools.partial(jax.ShapeDtypeStruct, dtype=jnp.float32)
    vmem = pl.BlockSpec(memory_space=pltpu.VMEM)

    base_levels = levels.astype(jnp.float32) / 255.0
    base = jnp.broadcast_to(base_levels[:, None], (labels, lanes))

    pairs = [(i, i ^ 1) for i in range(slabs)]
    across = [(i, i + 1) for i in range(1, slabs - 1, 2)]
    across += [(target, source) for source, target in across]
    other = lax.ppermute(volume, SLABS, across)
    pair = lax.ppermute(volume, SLABS, pairs)

    sent = pl.pallas_call(
        first_kernel,
        out_shape=f32((devices * ROWS, lanes)),
        in_specs=[vmem] * 4,
        out_specs=vmem,
        scratch_shapes=[
            pltpu.VMEM((labels, thick + 2, height, depth), jnp.float32),
            pltpu.VMEM((labels, 2, thick + 1, height, depth), jnp.float32),
        ],
        name="first",
    )(volume, pair, other, base)
    got = lax.all_to_all(sent.reshape(devices, 1, ROWS * lanes), AXES, 0, 0, tiled=True)
    got = got.reshape(devices * ROWS, lanes)

    layers = 3 * thick
    ahead, planes = pl.pallas_call(
        ahead_kernel,
        out_shape=[f32((labels, thick, height, depth)), f32((6, 8, lanes))],
        in_specs=[vmem] * 4,
        out_specs=[vmem] * 2,
        scratch_shapes=[
            pltpu.VMEM((labels, layers, height, depth), jnp.float32),
            pltpu.VMEM((labels, 3, layers, height, depth), jnp.float32),
            pltpu.VMEM((labels, layers, height, depth), jnp.float32),
        ],
        cost_estimate=pl.CostEstimate(
            flops=200 * labels * layers * height * depth,
            bytes_accessed=4 * 20 * height * depth,
            transcendentals=0,
        ),
        name="ahead",
    )(volume, pair, other, base)

    piece = f32((labels, thick, height // count, depth))
    sums, *pieces = pl.pallas_call(
        last_kernel,
        out_shape=[f32((devices, lanes))] + [piece] * count,
        in_specs=[vmem] * 5,
        out_specs=[vmem] * (count + 1),
        scratch_shapes=[pltpu.VMEM((labels, thick, height, depth), jnp.float32)],
        name="last",
    )(volume, ahead, planes, base, got)

    total = lax.all_to_all(sums.reshape(devices, 1, lanes), AXES, 0, 0, tiled=True)
    for shift in range(1, count):
        pieces[shift] = lax.ppermute(
            pieces[shift], "gy", [(i, i ^ shift) for i in range(count)]
        )
    labelling = pl.pallas_call(
        join_kernel,
        out_shape=f32((labels, thick * count, height // count, depth)),
        in_specs=[vmem] * count,
        out_specs=vmem,
        cost_estimate=pl.CostEstimate(
            flops=labels * thick * height * depth,
            bytes_accessed=8 * labels * thick * height * depth,
            transcendentals=0,
        ),
        name="join",
    )(*pieces)
    total = total.sum((0, 1))
    sizes_all, weighted_all = total[:labels], total[labels : 2 * labels]
    centers = (weighted_all + prior_weight * base_levels) / (sizes_all + prior_weight)
    return (labelling, centers)


def solution(mesh):
    return jax.shard_map(
        local,
        mesh=mesh,
        in_specs=(P(("gx", "gy"), None, "gz"), P()),
        out_specs=(P(None, "gx", "gy", "gz"), P()),
        check_vma=False,
    )
```

time: 160 us -> 41.3 us (0.26)
  blocking collectives: 85.9 us -> 0 us
  waiting for transfers between devices: 30.2 us -> 10 us
  other arithmetic: 12.8 us -> 1.29 us
  Pallas kernels: 0 us -> 9.98 us
  local copies, waits for them, and re-layouts: 7.36 us -> 1.88 us
  starting transfers between devices: 22 us -> 17.1 us
    psum x2 -> x0, blocking collectives: 85.9 us -> none  [local(): lax.psum((sizes_local, weighted), ('gx', 'gy', 'gz'))]
    ppermute x8 -> x5, waiting for transfers between devices: 30.2 us -> 0.46 us  [the longest x1 0.45 us: local(): pair = lax.ppermute(volume, SLABS, pairs)]
    ppermute x8 -> x5, starting transfers between devices: 18.1 us -> 6.98 us  [the longest x1 4.39 us: local(): pair = lax.ppermute(volume, SLABS, pairs)]
    pallas_call x0 -> x4, Pallas kernels: none -> 9.98 us  [the longest x1 3.41 us: local(): pl.pallas_call(ahead_kernel, out_shape=[f32((labels, thick, height, depth...]
    all_to_all x1 -> x2, waiting for transfers between devices: 0.01 us -> 9.54 us  [the longest x1 5.27 us: local(): lax.all_to_all(sums.reshape(devices, 1, lanes), AXES, 0, 0, tiled=True)]
    all_to_all x1 -> x2, starting transfers between devices: 3.9 us -> 10.1 us  [the longest x1 7.63 us: local(): lax.all_to_all(sent.reshape(devices, 1, ROWS * lanes), AXES, 0, 0, tiled=...]
    unnamed x36 -> x14, local copies, waits for them, and re-layouts: 4.51 us -> 1.28 us
    concatenate x4 -> x0, other arithmetic: 3.19 us -> none  [with_halo(): block = jnp.concatenate([low, block, high], axis=dim)]
  transfers between devices with their start and end apart: 9 -> 7, of which waited for: 5 -> 3; matrix products, arithmetic and copies ran while one was open for 0% -> 3% of each run, Pallas kernels for 0% -> 8%
where the time goes in v2:
time: 41.3 us; the launch traced here: 40.9 us
  starting transfers between devices  17.1 us (41%)
  waiting for transfers between devices  10 us (24%)
  Pallas kernels  9.98 us (24%)
  local copies, waits for them, and re-layouts  1.88 us (5%)
  other arithmetic  1.29 us (3%)
  between operations  0.69 us (2%)
    all_to_all x1, starting transfers between devices, local(): lax.all_to_all(sent.reshape(devices, 1, ROWS * lanes), AXES, 0, 0, tiled=...  7.63 us
    all_to_all x1, waiting for transfers between devices, local(): lax.all_to_all(sums.reshape(devices, 1, lanes), AXES, 0, 0, tiled=True)  5.27 us
    ppermute x1, starting transfers between devices, local(): pair = lax.ppermute(volume, SLABS, pairs)  4.39 us
    all_to_all x1, waiting for transfers between devices, local(): lax.all_to_all(sent.reshape(devices, 1, ROWS * lanes), AXES, 0, 0, tiled=...  4.27 us
    pallas_call x1, Pallas kernels, local(): pl.pallas_call(ahead_kernel, out_shape=[f32((labels, thick, height, depth...  3.41 us
    pallas_call x1, Pallas kernels, local(): pl.pallas_call(last_kernel, out_shape=[f32((devices, lanes))] + [piece] *...  2.59 us
    all_to_all x1, starting transfers between devices, local(): lax.all_to_all(sums.reshape(devices, 1, lanes), AXES, 0, 0, tiled=True)  2.48 us
    pallas_call x1, Pallas kernels, local(): pl.pallas_call(first_kernel, out_shape=f32((devices * ROWS, lanes)), in_s...  2.31 us
  transfers between devices with their start and end apart: 7, of which 3 were waited for; matrix products, arithmetic and copies ran while one was open for 3% of the time, Pallas kernels for 8%

profile of v2, /device:TPU:0, one launch (start us, length us, event | category | flops | bytes accessed | tf_op | source)
XLA Modules:
  0.0 40.9 jit_solution(7966987561655038960)
XLA Ops:
  0.6 0.7 %collective-permute-start.1 = (f32[2,64,128]{2,1,0:T(8,128)}, f32[2,64,128]{2,1,0:T(8,128)S(1)}, u32[]{:S(2)}, u32[]{:S(2)}) collective-permute-start(f32[2,64,128]{2,1,0:T(8,128)} %v_ref.5), channel_id=1, source_target_pairs={{4,8},{12,16},{20,24},{8,4},{16,12},{24,20},{5,9},{13,17},{21,25},... | collective-permute-start | bytes 196616 | tf_op jit(solution)/shard_map/ppermute | solution.py:451
  1.3 4.4 %collective-permute-start = (f32[2,64,128]{2,1,0:T(8,128)}, f32[2,64,128]{2,1,0:T(8,128)S(1)}, u32[]{:S(2)}, u32[]{:S(2)}) collective-permute-start(f32[2,64,128]{2,1,0:T(8,128)} %v_ref.5), channel_id=1, source_target_pairs={{0,4},{4,0},{8,12},{12,8},{16,20},{20,16},{24,28},{28,24},{1,5},{5... | collective-permute-start | bytes 196616 | tf_op jit(solution)/shard_map/ppermute | solution.py:452
  5.7 0.7 %convert_multiply_fusion = f32[4]{0:T(128)S(1)} fusion(s32[4]{0:T(128)} %param.3), kind=kLoop, calls=%fused_computation.1 | loop fusion | flops 8 | bytes 32 | tf_op jit(solution)/shard_map/div | solution.py:445
  6.4 0.0 collective-permute-done.1.other_ref
  6.4 0.0 copy-start.1
  6.4 0.4 %collective-permute-done.pair_ref = f32[2,64,128]{2,1,0:T(8,128)S(1)} collective-permute-done((f32[2,64,128]{2,1,0:T(8,128)}, f32[2,64,128]{2,1,0:T(8,128)S(1)}, u32[]{:S(2)}, u32[]{:S(2)}) %collective-permute-start) | collective-permute-done | bytes 65568 | tf_op jit(solution)/shard_map/ppermute | solution.py:452
  6.8 0.6 %broadcast_in_dim.2.base_ref = f32[4,128]{1,0:T(4,128)} broadcast(f32[4]{0:T(128)S(1)} %convert_multiply_fusion), dimensions={0} | broadcast | bytes 2064 | tf_op jit(solution)/shard_map/broadcast_in_dim | solution.py:446
  7.4 0.0 copy-done.1
  7.4 0.0 copy-done.2
  7.4 2.3 %first.1 = f32[160,128]{1,0:T(8,128)} custom-call(f32[2,64,128]{2,1,0:T(8,128)} %v_ref.5, f32[2,64,128]{2,1,0:T(8,128)} %copy-done.2, f32[2,64,128]{2,1,0:T(8,128)} %copy-done.1, f32[4,128]{1,0:T(4,128)} %broadcast_in_dim.2.base_ref), custom_call_target="tpu_custom_call" | custom-call | tf_op jit(solution)/shard_map/first/pallas_call | solution.py:454
  9.7 7.6 %all-to-all-start = ((f32[32,1,640]{2,1,0:T(1,128)}), f32[32,1,640]{2,1,0:T(1,128)S(1)}, u32[]{:S(2)}, u32[]{:S(2)}) async-start(f32[32,1,640]{2,1,0:T(1,128)} %bitcast.6), calls=%async_computation | async-start | bytes 163840 | tf_op jit(solution)/shard_map/all_to_all | solution.py:465
  17.4 3.4 %ahead.1 = (f32[4,2,64,128]{3,2,1,0:T(8,128)}, f32[6,8,128]{2,1,0:T(8,128)}) custom-call(f32[2,64,128]{2,1,0:T(8,128)} %v_ref.5, f32[2,64,128]{2,1,0:T(8,128)} %copy-done.2, f32[2,64,128]{2,1,0:T(8,128)} %copy-done.1, f32[4,128]{1,0:T(4,128)} %broadcast_in_dim.2.base_ref), custom_call_target="tpu_custom_call" | custom-call | flops 39321600 | bytes 655360 | tf_op jit(solution)/shard_map/ahead/pallas_call | solution.py:469
  20.8 4.3 %all-to-all-done = f32[32,1,640]{2,1,0:T(1,128)S(1)} async-done(((f32[32,1,640]{2,1,0:T(1,128)}), f32[32,1,640]{2,1,0:T(1,128)S(1)}, u32[]{:S(2)}, u32[]{:S(2)}) %all-to-all-start) | async-done | bytes 81952 | tf_op jit(solution)/shard_map/all_to_all | solution.py:465
  25.1 0.6 %copy-done = f32[32,1,640]{2,1,0:T(1,128)} copy-done((f32[32,1,640]{2,1,0:T(1,128)}, f32[32,1,640]{2,1,0:T(1,128)S(1)}, u32[]{:S(2)}) %copy-start) | copy-done | bytes 81944
  25.7 2.6 %last.1 = (f32[32,128]{1,0:T(8,128)}, f32[4,2,16,128]{3,2,1,0:T(8,128)}, f32[4,2,16,128]{3,2,1,0:T(8,128)}, f32[4,2,16,128]{3,2,1,0:T(8,128)}, f32[4,2,16,128]{3,2,1,0:T(8,128)}) custom-call(f32[2,64,128]{2,1,0:T(8,128)} %v_ref.5, f32[4,2,64,128]{3,2,1,0:T(8,128)} %get-tuple-element.9.w_ref, f32[6,8,128]{2,1,0:T(8,128)} %get-tuple-element.10.q_ref, ...), custom_call_target="tpu_custom_call" | custom-call | tf_op jit(solution)/shard_map/last/pallas_call | solution.py:488
  28.3 2.5 %all-to-all-start.1 = ((f32[32,1,128]{2,1,0:T(1,128)}), f32[32,1,128]{2,1,0:T(1,128)S(1)}, u32[]{:S(2)}, u32[]{:S(2)}) async-start(f32[32,1,128]{2,1,0:T(1,128)} %bitcast.7), calls=%async_computation.1 | async-start | bytes 32768 | tf_op jit(solution)/shard_map/all_to_all | solution.py:497
  30.8 0.2 collective-permute-start.2
  30.9 1.6 %collective-permute-start.3 = (f32[4,2,16,128]{3,2,1,0:T(8,128)}, f32[4,2,16,128]{3,2,1,0:T(8,128)S(1)}, u32[]{:S(2)}, u32[]{:S(2)}) collective-permute-start(f32[4,2,16,128]{3,2,1,0:T(8,128)} %get-tuple-element.13), channel_id=1, source_target_pairs={{0,8},{4,12},{8,0},{12,4},{1,9},{5,13},{9,1},{13,5},{2,10},{6,14},... | collective-permute-start | bytes 196616 | tf_op jit(solution)/shard_map/ppermute | solution.py:499
  32.6 0.1 collective-permute-start.4
  32.7 5.3 %all-to-all-done.1 = f32[32,1,128]{2,1,0:T(1,128)S(1)} async-done(((f32[32,1,128]{2,1,0:T(1,128)}), f32[32,1,128]{2,1,0:T(1,128)S(1)}, u32[]{:S(2)}, u32[]{:S(2)}) %all-to-all-start.1) | async-done | bytes 16416 | tf_op jit(solution)/shard_map/all_to_all | solution.py:497
  38.0 0.1 reduce_sum.9
  38.0 0.0 copy-done.6
  38.0 0.6 %add_divide_fusion = f32[4]{0:T(128)} fusion(f32[128]{0:T(128)S(1)} %reduce_sum.9, s32[4]{0:T(128)S(1)} %copy-done.6), kind=kLoop, calls=%fused_computation | loop fusion | flops 20 | bytes 64 | tf_op jit(solution)/shard_map/div | solution.py:516
  38.6 0.0 collective-permute-done.2.refs_1_
  38.6 0.0 collective-permute-done.3.refs_2_
  38.6 0.0 copy-start.4
  38.6 0.0 collective-permute-done.4.refs_3_
  38.6 0.0 copy-start.5
  38.6 0.6 %copy-done.3 = f32[4,2,16,128]{3,2,1,0:T(8,128)} copy-done((f32[4,2,16,128]{3,2,1,0:T(8,128)}, f32[4,2,16,128]{3,2,1,0:T(8,128)S(1)}, u32[]{:S(2)}) %copy-start.3) | copy-done | bytes 65560
  39.2 0.0 copy-done.4
  39.2 0.0 copy-done.5
  39.3 1.7 %join.1 = f32[4,8,16,128]{3,2,1,0:T(8,128)} custom-call(f32[4,2,16,128]{3,2,1,0:T(8,128)} %get-tuple-element.11.refs_0_, f32[4,2,16,128]{3,2,1,0:T(8,128)} %copy-done.3, f32[4,2,16,128]{3,2,1,0:T(8,128)} %copy-done.4, f32[4,2,16,128]{3,2,1,0:T(8,128)} %copy-done.5), custom_call_target="tpu_custom_call" | custom-call | flops 65536 | bytes 524288 | tf_op jit(solution)/shard_map/join/pallas_call | solution.py:502
  (4 shorter events, 0.0 us)
Async XLA Ops:
  0.6 5.7 %collective-permute-start.1 = (f32[2,64,128]{2,1,0:T(8,128)}, f32[2,64,128]{2,1,0:T(8,128)S(1)}, u32[]{:S(2)}, u32[]{:S(2)}) collective-permute-start(f32[2,64,128]{2,1,0:T(8,128)} %v_ref.5), channel_id=1, source_target_pairs={{4,8},{12,16},{20,24},{8,4},{16,12},{24,20},{5,9},{13,17},{21,25},... | collective-permute-start | bytes 196616 | tf_op jit(solution)/shard_map/ppermute | solution.py:451
  1.3 5.5 %collective-permute-start = (f32[2,64,128]{2,1,0:T(8,128)}, f32[2,64,128]{2,1,0:T(8,128)S(1)}, u32[]{:S(2)}, u32[]{:S(2)}) collective-permute-start(f32[2,64,128]{2,1,0:T(8,128)} %v_ref.5), channel_id=1, source_target_pairs={{0,4},{4,0},{8,12},{12,8},{16,20},{20,16},{24,28},{28,24},{1,5},{5... | collective-permute-start | bytes 196616 | tf_op jit(solution)/shard_map/ppermute | solution.py:452
  6.4 1.1 %copy-start.1 = (f32[2,64,128]{2,1,0:T(8,128)}, f32[2,64,128]{2,1,0:T(8,128)S(1)}, u32[]{:S(2)}) copy-start(f32[2,64,128]{2,1,0:T(8,128)S(1)} %collective-permute-done.1.other_ref) | copy-start | bytes 196612
  6.8 0.6 %copy-start.2 = (f32[2,64,128]{2,1,0:T(8,128)}, f32[2,64,128]{2,1,0:T(8,128)S(1)}, u32[]{:S(2)}) copy-start(f32[2,64,128]{2,1,0:T(8,128)S(1)} %collective-permute-done.pair_ref) | copy-start | bytes 196612
  9.7 15.3 %all-to-all-start = ((f32[32,1,640]{2,1,0:T(1,128)}), f32[32,1,640]{2,1,0:T(1,128)S(1)}, u32[]{:S(2)}, u32[]{:S(2)}) async-start(f32[32,1,640]{2,1,0:T(1,128)} %bitcast.6), calls=%async_computation | async-start | bytes 163840 | tf_op jit(solution)/shard_map/all_to_all | solution.py:465
  25.1 0.6 %copy-start = (f32[32,1,640]{2,1,0:T(1,128)}, f32[32,1,640]{2,1,0:T(1,128)S(1)}, u32[]{:S(2)}) copy-start(f32[32,1,640]{2,1,0:T(1,128)S(1)} %all-to-all-done) | copy-start | bytes 245764
  28.3 9.7 %all-to-all-start.1 = ((f32[32,1,128]{2,1,0:T(1,128)}), f32[32,1,128]{2,1,0:T(1,128)S(1)}, u32[]{:S(2)}, u32[]{:S(2)}) async-start(f32[32,1,128]{2,1,0:T(1,128)} %bitcast.7), calls=%async_computation.1 | async-start | bytes 32768 | tf_op jit(solution)/shard_map/all_to_all | solution.py:497
  30.8 7.8 %collective-permute-start.2 = (f32[4,2,16,128]{3,2,1,0:T(8,128)}, f32[4,2,16,128]{3,2,1,0:T(8,128)S(1)}, u32[]{:S(2)}, u32[]{:S(2)}) collective-permute-start(f32[4,2,16,128]{3,2,1,0:T(8,128)} %get-tuple-element.12), channel_id=1, source_target_pairs={{0,4},{4,0},{8,12},{12,8},{1,5},{5,1},{9,13},{13,9},{2,6},{6,2},{1... | collective-permute-start | bytes 196616 | tf_op jit(solution)/shard_map/ppermute | solution.py:499
  30.9 7.7 %collective-permute-start.3 = (f32[4,2,16,128]{3,2,1,0:T(8,128)}, f32[4,2,16,128]{3,2,1,0:T(8,128)S(1)}, u32[]{:S(2)}, u32[]{:S(2)}) collective-permute-start(f32[4,2,16,128]{3,2,1,0:T(8,128)} %get-tuple-element.13), channel_id=1, source_target_pairs={{0,8},{4,12},{8,0},{12,4},{1,9},{5,13},{9,1},{13,5},{2,10},{6,14},... | collective-permute-start | bytes 196616 | tf_op jit(solution)/shard_map/ppermute | solution.py:499
  32.6 5.4 %copy-start.6 = (s32[4]{0:T(128)S(1)}, s32[4]{0:T(128)}, u32[]{:S(2)}) copy-start(s32[4]{0:T(128)} %param.3) | copy-start | bytes 52
  32.6 6.0 %collective-permute-start.4 = (f32[4,2,16,128]{3,2,1,0:T(8,128)}, f32[4,2,16,128]{3,2,1,0:T(8,128)S(1)}, u32[]{:S(2)}, u32[]{:S(2)}) collective-permute-start(f32[4,2,16,128]{3,2,1,0:T(8,128)} %get-tuple-element.14), channel_id=1, source_target_pairs={{0,12},{4,8},{8,4},{12,0},{1,13},{5,9},{9,5},{13,1},{2,14},{6,10},... | collective-permute-start | bytes 196616 | tf_op jit(solution)/shard_map/ppermute | solution.py:499
  38.6 0.6 %copy-start.3 = (f32[4,2,16,128]{3,2,1,0:T(8,128)}, f32[4,2,16,128]{3,2,1,0:T(8,128)S(1)}, u32[]{:S(2)}) copy-start(f32[4,2,16,128]{3,2,1,0:T(8,128)S(1)} %collective-permute-done.2.refs_1_) | copy-start | bytes 196612
  38.6 0.6 %copy-start.4 = (f32[4,2,16,128]{3,2,1,0:T(8,128)}, f32[4,2,16,128]{3,2,1,0:T(8,128)S(1)}, u32[]{:S(2)}) copy-start(f32[4,2,16,128]{3,2,1,0:T(8,128)S(1)} %collective-permute-done.3.refs_2_) | copy-start | bytes 196612
  38.6 0.6 %copy-start.5 = (f32[4,2,16,128]{3,2,1,0:T(8,128)}, f32[4,2,16,128]{3,2,1,0:T(8,128)S(1)}, u32[]{:S(2)}) copy-start(f32[4,2,16,128]{3,2,1,0:T(8,128)S(1)} %collective-permute-done.4.refs_3_) | copy-start | bytes 196612

commit v3 on v2

v3 whole, which is shorter than its diff:
```python
import functools

import jax
import jax.numpy as jnp
from jax import lax
from jax.experimental import pallas as pl
from jax.experimental.pallas import tpu as pltpu
from jax.sharding import PartitionSpec as P


tau_step = 0.25
prior_weight = 1.0


AXES = ("gx", "gy", "gz")
SLABS = ("gx", "gy")
ROWS = 5


def project_simplex(values, total):
    a, b, c, d = values
    a, b = jnp.maximum(a, b), jnp.minimum(a, b)
    c, d = jnp.maximum(c, d), jnp.minimum(c, d)
    a, c = jnp.maximum(a, c), jnp.minimum(a, c)
    b, d = jnp.maximum(b, d), jnp.minimum(b, d)
    b, c = jnp.maximum(b, c), jnp.minimum(b, c)
    one = a - total
    two = one + b
    three = two + c
    four = three + d
    threshold = jnp.maximum(
        jnp.maximum(one, two * 0.5), jnp.maximum(three * (1.0 / 3.0), four * 0.25)
    )
    return [jnp.maximum(value - threshold, 0.0) for value in values]


def affine(centers, unit):
    return [
        (center * (2.0 * unit * tau_step), center * center * (unit * tau_step))
        for center in centers
    ]


def attraction(volume, terms):
    return [volume * slope - offset for slope, offset in terms]


def shrink_of(x, y, z):
    return lax.rsqrt(jnp.maximum(x * x + y * y + z * z, 1.0))


class Planes:
    def __init__(self, shape, height, x_first, x_total):
        self.height = height
        self.rows, self.lanes = shape
        lane = lax.broadcasted_iota(jnp.int32, shape, 1)
        self.low = lane < height
        y = jnp.where(self.low, lane, lane - height)
        x = x_first + jnp.where(self.low, 0, 1)
        self.open_x = (x != x_total - 1).astype(jnp.float32)
        self.open_y = (y != height - 1).astype(jnp.float32)
        self.inside = (x >= 0).astype(jnp.float32)

    def dual(self, value, next_z, old=None):
        swapped = pltpu.roll(value, self.height, 1)
        following = jnp.where(self.low, swapped, pltpu.roll(swapped, self.rows - 1, 0))
        x = (following - value) * self.open_x
        y = (pltpu.roll(value, self.lanes - 1, 1) - value) * self.open_y
        z = next_z - value
        if old is not None:
            x, y, z = old[0] + x, old[1] + y, old[2] + z
        shrink = shrink_of(x, y, z)
        return x * shrink, y * shrink, z * shrink

    def behind_xy(self, x, y):
        swapped = pltpu.roll(x, self.height, 1)
        before_x = jnp.where(self.low, pltpu.roll(swapped, 1, 0), swapped)
        return (x - before_x) + (y - pltpu.roll(y, 1, 1))


def total_of(value):
    return jnp.sum(jnp.sum(value, axis=0, keepdims=True), axis=1, keepdims=True)


def base_kernel(levels_ref, base_ref):
    values = levels_ref[...].astype(jnp.float32) / 255.0
    for label in range(values.shape[1]):
        base_ref[label : label + 1] = jnp.broadcast_to(
            values[:, label : label + 1], (1, base_ref.shape[1])
        )


def base_of(base_ref):
    return [base_ref[label : label + 1] for label in range(base_ref.shape[0])]


def pack_sums(sums, shape):
    lane = lax.broadcasted_iota(jnp.int32, shape, 1)
    row = jnp.zeros(shape, jnp.float32)
    for index, value in enumerate(sums):
        row = jnp.where(lane == index, total_of(value), row)
    return row


def slab_index():
    return lax.axis_index("gx") * lax.axis_size("gy") + lax.axis_index("gy")


def open_lanes(depth):
    lane = lax.broadcasted_iota(jnp.int32, (1, depth), 1)
    return (lane != depth - 1).astype(jnp.float32)


def volume_layers(v_ref, pair_ref, other_ref, halo):
    thick = v_ref.shape[0]
    odd = lax.rem(slab_index(), 2) == 1

    def read(layer, rows=slice(None)):
        if layer < halo:
            layer += thick - halo
            return jnp.where(odd, pair_ref[layer, rows], other_ref[layer, rows])
        layer -= halo
        if layer < thick:
            return v_ref[layer, rows]
        layer -= thick
        return jnp.where(odd, other_ref[layer, rows], pair_ref[layer, rows])

    return read


def add_to(sums, index, term):
    sums[index] = term if sums[index] is None else sums[index] + term


CHUNK = 16
BASE_FLOPS = 50_000_000


def store_padded(ref, where, start, value, height):
    rows = value.shape[0]
    ref[where + (slice(start, start + rows),)] = value
    if start + rows == height:
        ref[where + (slice(height, height + 1),)] = value[rows - 1 :]


def first_halves(read, layers, height, terms, h_ref):
    for layer in layers:
        for start in range(0, height, CHUNK):
            values = read(layer, slice(start, start + CHUNK))
            for label, half in enumerate(project_simplex(attraction(values, terms), 0.5)):
                store_padded(h_ref, (label, layer), start, half, height)


def gradient(h_ref, label, layer, height, depth, open_z):
    half = h_ref[label, layer, 0:height]
    x = h_ref[label, layer + 1, 0:height] - half
    y = h_ref[label, layer, 1 : height + 1] - half
    z = (pltpu.roll(half, depth - 1, 1) - half) * open_z
    return x, y, z


def behind_yz(y, z, y_ref, where, height):
    y_ref[where + (slice(0, 8),)] = jnp.zeros((8, y.shape[1]), jnp.float32)
    y_ref[where + (slice(8, 8 + height),)] = y
    return (y - y_ref[where + (slice(7, 7 + height),)]) + (z - pltpu.roll(z, 1, 1))


def first_kernel(
    v_hbm, pair_ref, other_ref, base_ref, out_ref, v_ref, h_ref, y_ref, divergence_ref, arrived
):
    copy = pltpu.make_async_copy(v_hbm, v_ref, arrived)
    copy.start()
    slabs = lax.axis_size(SLABS)
    blocks = lax.axis_size("gz")
    slab, block = slab_index(), lax.axis_index("gz")
    thick, height, depth = v_hbm.shape
    lanes = thick * height
    devices = slabs * blocks
    labels = base_ref.shape[0]
    terms = affine(base_of(base_ref), 0.5)
    open_z = open_lanes(depth)
    read = volume_layers(v_ref, pair_ref, other_ref, 1)

    first_halves(read, (0, thick + 1), height, terms, h_ref)
    copy.wait()
    first_halves(read, range(1, thick + 1), height, terms, h_ref)
    turned = jnp.transpose(v_ref[...].reshape(lanes, depth))
    for row, plane in enumerate((0, 1, depth - 2, depth - 1)):
        out_ref[pl.ds(row, devices, stride=ROWS), :] = jnp.broadcast_to(
            turned[plane : plane + 1], (devices, lanes)
        )
    inside = (slab > 0).astype(jnp.float32)
    open_x = (slab < slabs - 1).astype(jnp.float32)
    for label in range(labels):
        before = None
        for layer in range(thick + 1):
            x, y, z = gradient(h_ref, label, layer, height, depth, open_z)
            if layer == thick:
                x = x * open_x
            shrink = shrink_of(x, y, z)
            x = x * shrink
            if layer == 0:
                x = x * inside
            else:
                where = (label, layer - 1)
                divergence_ref[where] = (x - before) + behind_yz(
                    y * shrink, z * shrink, y_ref, where, height
                )
            before = x
    sums = [None] * (2 * labels)
    for layer in range(thick):
        for start in range(0, height, CHUNK):
            rows = slice(start, start + CHUNK)
            values = v_ref[layer, rows]
            entries = [
                h_ref[label, layer + 1, rows] + 0.0625 * divergence_ref[label, layer, rows] + term
                for label, term in enumerate(attraction(values, terms))
            ]
            for label, value in enumerate(project_simplex(entries, 0.5)):
                add_to(sums, label, value)
                add_to(sums, labels + label, value * values)
    lane = lax.broadcasted_iota(jnp.int32, (CHUNK, depth), 1)
    first = jnp.where(block > 0, 0, -1)
    last = jnp.where(block < blocks - 1, depth - 1, depth)
    keep = (lane != first) & (lane != last)
    sums = [jnp.where(keep, value, 0.0) for value in sums]
    out_ref[pl.ds(ROWS - 1, devices, stride=ROWS), :] = jnp.broadcast_to(
        pack_sums(sums, (1, lanes)), (devices, lanes)
    )


def ahead_kernel(
    v_ref, pair_ref, other_ref, base_ref, w_ref, q_ref, h_ref, s_ref, dual_ref, y_ref, l_ref
):
    slabs = lax.axis_size(SLABS)
    slab = slab_index()
    thick, height, depth = v_ref.shape
    lanes = thick * height
    labels = base_ref.shape[0]
    terms = affine(base_of(base_ref), 0.5)
    open_z = open_lanes(depth)
    halo = thick
    layers = thick + 2 * halo
    read = volume_layers(v_ref, pair_ref, other_ref, halo)

    first_halves(read, range(layers), height, terms, h_ref)
    inside = (slab > 0).astype(jnp.float32)
    open_x = (slab < slabs - 1).astype(jnp.float32)
    end = halo + thick - 1
    for label in range(labels):
        before = None
        for layer in range(layers - 1):
            x, y, z = gradient(h_ref, label, layer, height, depth, open_z)
            if layer == end:
                x = x * open_x
            shrink = shrink_of(x, y, z)
            x = x * shrink
            if layer == halo - 1:
                x = x * inside
            if layer:
                y, z = y * shrink, z * shrink
                where = (label, layer)
                dual_ref[label, 0, layer] = x
                dual_ref[label, 1, layer] = y
                dual_ref[label, 2, layer] = z
                l_ref[where] = (x - before) + behind_yz(y, z, y_ref, where, height)
            before = x
    for layer in range(1, layers - 1):
        for start in range(0, height, CHUNK):
            rows = slice(start, start + CHUNK)
            values = read(layer, rows)
            halves = [h_ref[label, layer, rows] for label in range(labels)]
            entries = [
                halves[label] + 0.0625 * l_ref[label, layer, rows] + term
                for label, term in enumerate(attraction(values, terms))
            ]
            for label, value in enumerate(project_simplex(entries, 0.5)):
                value = value + value
                store_padded(s_ref, (label, layer), start, value - halves[label], height)
                l_ref[label, layer, rows] = value
    for label in range(labels):
        before = None
        for layer in range(halo - 1, halo + thick):
            x, y, z = gradient(s_ref, label, layer, height, depth, open_z)
            if layer == end:
                x = x * open_x
            x = dual_ref[label, 0, layer] + x
            y = dual_ref[label, 1, layer] + y
            z = dual_ref[label, 2, layer] + z
            shrink = shrink_of(x, y, z)
            x = x * shrink
            if layer == halo - 1:
                x = x * inside
            else:
                divergence = (x - before) + behind_yz(
                    y * shrink, z * shrink, y_ref, (label, layer), height
                )
                w_ref[label, layer - halo] = l_ref[label, layer] + 0.125 * divergence
            before = x
    row = lax.broadcasted_iota(jnp.int32, (8, lanes), 0)
    near, far = [], []
    for start in (0, halo, halo + thick):
        turned = jnp.transpose(
            jnp.concatenate([read(start + index) for index in range(thick)], axis=0)
        )
        near.append(turned[0:8])
        far.append(turned[depth - 8 : depth])
    for column in range(6):
        plane = jnp.zeros((8, lanes), jnp.float32)
        for which in range(3):
            if column >= 2:
                plane = jnp.where(row == which, near[which][column - 2 : column - 1], plane)
            if column < 4:
                plane = jnp.where(row == 4 + which, far[which][4 + column : 5 + column], plane)
        q_ref[column] = plane


def last_kernel(v_ref, w_ref, q_ref, base_ref, got_ref, sums_ref, *rest):
    slabs = lax.axis_size(SLABS)
    blocks = lax.axis_size("gz")
    count = lax.axis_size("gy")
    slab, block = slab_index(), lax.axis_index("gz")
    pieces, lab_ref = rest[:count], rest[count]
    thick, height, depth = v_ref.shape
    lanes = thick * height
    labels = base_ref.shape[0]
    base = base_of(base_ref)
    terms = affine(base, 0.5)
    devices = slabs * blocks
    x_total = slabs * thick

    row = lax.broadcasted_iota(jnp.int32, (slabs, lanes), 0)
    everywhere = Planes((slabs, lanes), height, thick * row, x_total)
    sums = [None] * (2 * labels)
    for end in range(blocks - 1):
        planes = [
            got_ref[pl.ds((end + beyond) * ROWS + which, slabs, stride=blocks * ROWS), :]
            for beyond, which in ((0, 2), (0, 3), (1, 0), (1, 1))
        ]
        pulls = [attraction(plane, terms) for plane in planes]
        first = [project_simplex(pull, 0.5) for pull in pulls]
        divergence = [[], []]
        for label in range(labels):
            duals = [
                everywhere.dual(first[index][label], first[index + 1][label])
                for index in range(3)
            ]
            for index in (1, 2):
                x, y, z = duals[index]
                divergence[index - 1].append(
                    everywhere.behind_xy(x, y) + (z - duals[index - 1][2])
                )
        for index in (1, 2):
            entries = [
                first[index][label] + 0.0625 * divergence[index - 1][label] + pulls[index][label]
                for label in range(labels)
            ]
            for label, value in enumerate(project_simplex(entries, 0.5)):
                add_to(sums, label, value)
                add_to(sums, labels + label, value * planes[index])
    parts = got_ref[pl.ds(ROWS - 1, devices, stride=ROWS), :]
    lane = lax.broadcasted_iota(jnp.int32, (1, lanes), 1)
    parts = jnp.sum(parts, axis=0, keepdims=True)
    if blocks > 1:
        parts = parts + pack_sums(sums, (1, lanes))
    whole = [
        2.0 * jnp.sum(jnp.where(lane == index, parts, 0.0), axis=1, keepdims=True)
        for index in range(2 * labels)
    ]
    centers = [
        (whole[labels + label] + prior_weight * base[label]) / (whole[label] + prior_weight)
        for label in range(labels)
    ]

    row = lax.broadcasted_iota(jnp.int32, (8, lanes), 0)
    local = Planes((8, lanes), height, thick * (slab - 1 + (row & 3)), x_total)
    planes = [q_ref[column] for column in range(6)]
    for which in range(3):
        index = jnp.clip(slab - 1 + which, 0, slabs - 1) * blocks
        low = (index + jnp.maximum(block - 1, 0)) * ROWS
        high = (index + jnp.minimum(block + 1, blocks - 1)) * ROWS
        for column in range(2):
            source = got_ref[pl.ds(low + 2 + column, 1), :]
            planes[column] = jnp.where(row == which, source, planes[column])
            source = got_ref[pl.ds(high + column, 1), :]
            planes[4 + column] = jnp.where(row == 4 + which, source, planes[4 + column])
    pulls = [attraction(plane, terms) for plane in planes]
    first = [project_simplex(pull, 0.5) for pull in pulls]
    duals = []
    for label in range(labels):
        duals.append([])
        for column in range(5):
            x, y, z = local.dual(first[column][label], first[column + 1][label])
            duals[label].append((x * local.inside, y, z))
    second, smooth = {}, {}
    for column in range(1, 5):
        entries = []
        for label in range(labels):
            x, y, z = duals[label][column]
            divergence = local.behind_xy(x, y) + (z - duals[label][column - 1][2])
            entries.append(first[column][label] + 0.0625 * divergence + pulls[column][label])
        second[column] = [value + value for value in project_simplex(entries, 0.5)]
        smooth[column] = [
            second[column][label] - first[column][label] for label in range(labels)
        ]
    for label in range(labels):
        for column in range(1, 4):
            x, y, z = local.dual(
                smooth[column][label], smooth[column + 1][label], duals[label][column]
            )
            duals[label][column] = (x * local.inside, y, z)
    terms = affine(centers, 1.0)
    edge = {}
    for column in (2, 3):
        pull = attraction(planes[column], terms)
        entries = []
        for label in range(labels):
            x, y, z = duals[label][column]
            divergence = local.behind_xy(x, y) + (z - duals[label][column - 1][2])
            entries.append(second[column][label] + 0.125 * divergence + pull[label])
        edge[column] = project_simplex(entries, 1.0)
    step = depth // labels
    tiles = [jnp.zeros((8, lanes), jnp.float32) for _ in range(depth // 8)]
    for label in range(labels):
        two, three = edge[2][label], edge[3][label]
        place = label * step // 8
        tiles[place] = tiles[place] + jnp.where(
            row == 0, pltpu.roll(two, 7, 0), jnp.where(row == 1, three, 0.0)
        )
        place = (place - 1) % (depth // 8)
        tiles[place] = tiles[place] + jnp.where(
            row == 6, pltpu.roll(two, 1, 0), jnp.where(row == 7, pltpu.roll(three, 2, 0), 0.0)
        )
    columns = jnp.transpose(jnp.concatenate(tiles, axis=0))

    z = lax.broadcasted_iota(jnp.int32, (CHUNK, depth), 1)
    replaced = ((z < 2) & (block > 0)) | ((z >= depth - 2) & (block < blocks - 1))
    sums = [None] * (2 * labels)
    for layer in range(thick):
        for start in range(0, height, CHUNK):
            rows = slice(start, start + CHUNK)
            values = v_ref[layer, rows]
            entries = [
                w_ref[label, layer, rows] + pull
                for label, pull in enumerate(attraction(values, terms))
            ]
            for label, value in enumerate(project_simplex(entries, 1.0)):
                column = columns[layer * height + start : layer * height + start + CHUNK]
                if label:
                    column = pltpu.roll(column, depth - label * step, 1)
                value = jnp.where(replaced, column, value)
                lab_ref[label, layer, rows] = value
                add_to(sums, label, value)
                add_to(sums, labels + label, value * values)
    sums_ref[...] = jnp.broadcast_to(pack_sums(sums, (1, lanes)), (devices, lanes))
    rows = height // count
    me = lax.axis_index("gy")
    for other in range(count):
        start = pl.multiple_of((me ^ other) * rows, rows)
        pieces[other][...] = lab_ref[:, :, pl.ds(start, rows), :]


def join_kernel(*refs):
    *pieces, out_ref = refs
    me = lax.axis_index("gy")
    thick = pieces[0].shape[1]
    for other, piece in enumerate(pieces):
        out_ref[:, pl.ds((me ^ other) * thick, thick)] = piece[...]


def local(volume, levels):
    slabs = lax.axis_size(SLABS)
    blocks = lax.axis_size("gz")
    count = lax.axis_size("gy")
    devices = slabs * blocks
    thick, height, depth = volume.shape
    labels = levels.shape[0]
    lanes = thick * height
    if thick != 2 or labels != 4 or count & (count - 1):
        raise ValueError("unsupported sizes")
    f32 = functools.partial(jax.ShapeDtypeStruct, dtype=jnp.float32)
    vmem = pl.BlockSpec(memory_space=pltpu.VMEM)

    base_levels = levels.astype(jnp.float32) / 255.0
    params = pltpu.CompilerParams(vmem_limit_bytes=8 << 20)
    base = pl.pallas_call(
        base_kernel,
        out_shape=f32((labels, lanes)),
        in_specs=[vmem],
        out_specs=vmem,
        compiler_params=params,
        cost_estimate=pl.CostEstimate(flops=BASE_FLOPS, bytes_accessed=0, transcendentals=0),
        name="base",
    )(levels.reshape(1, labels))

    pairs = [(i, i ^ 1) for i in range(slabs)]
    across = [(i, i + 1) for i in range(1, slabs - 1, 2)]
    across += [(target, source) for source, target in across]
    pair = lax.ppermute(volume, SLABS, pairs)
    other = lax.ppermute(volume, SLABS, across)

    sent, volume = pl.pallas_call(
        first_kernel,
        out_shape=[f32((devices * ROWS, lanes)), f32(volume.shape)],
        in_specs=[pl.BlockSpec(memory_space=pltpu.HBM)] + [vmem] * 3,
        out_specs=[vmem] * 2,
        scratch_shapes=[
            pltpu.VMEM((labels, thick + 2, height + 8, depth), jnp.float32),
            pltpu.VMEM((labels, thick, height + 8, depth), jnp.float32),
            pltpu.VMEM((labels, thick, height, depth), jnp.float32),
            pltpu.SemaphoreType.DMA,
        ],
        compiler_params=params,
        name="first",
    )(volume, pair, other, base)
    got = lax.all_to_all(sent.reshape(devices, 1, ROWS * lanes), AXES, 0, 0, tiled=True)
    got = got.reshape(devices * ROWS, lanes)

    layers = 3 * thick
    ahead, planes = pl.pallas_call(
        ahead_kernel,
        out_shape=[f32((labels, thick, height, depth)), f32((6, 8, lanes))],
        in_specs=[vmem] * 4,
        out_specs=[vmem] * 2,
        scratch_shapes=[
            pltpu.VMEM((labels, layers, height + 8, depth), jnp.float32),
            pltpu.VMEM((labels, layers, height + 8, depth), jnp.float32),
            pltpu.VMEM((labels, 3, layers, height, depth), jnp.float32),
            pltpu.VMEM((labels, layers, height + 8, depth), jnp.float32),
            pltpu.VMEM((labels, layers, height, depth), jnp.float32),
        ],
        cost_estimate=pl.CostEstimate(
            flops=200 * labels * layers * height * depth,
            bytes_accessed=4 * 20 * height * depth,
            transcendentals=0,
        ),
        compiler_params=params,
        name="ahead",
    )(volume, pair, other, base)

    piece = f32((labels, thick, height // count, depth))
    sums, *pieces = pl.pallas_call(
        last_kernel,
        out_shape=[f32((devices, lanes))] + [piece] * count,
        in_specs=[vmem] * 5,
        out_specs=[vmem] * (count + 1),
        scratch_shapes=[pltpu.VMEM((labels, thick, height, depth), jnp.float32)],
        compiler_params=params,
        name="last",
    )(volume, ahead, planes, base, got)

    total = lax.all_to_all(sums.reshape(devices, 1, lanes), AXES, 0, 0, tiled=True)
    for shift in range(1, count):
        pieces[shift] = lax.ppermute(pieces[shift], "gy", [(i, i ^ shift) for i in range(count)])
    join = pl.pallas_call(
        join_kernel,
        out_shape=f32((labels, thick * count, height // count, depth)),
        in_specs=[vmem] * count,
        out_specs=vmem,
        cost_estimate=pl.CostEstimate(
            flops=labels * thick * height * depth,
            bytes_accessed=8 * labels * thick * height * depth,
            transcendentals=0,
        ),
        compiler_params=params,
        name="join",
    )
    labelling = join(*pieces)
    total = total.sum((0, 1))
    sizes_all, weighted_all = total[:labels], total[labels : 2 * labels]
    centers = (weighted_all + prior_weight * base_levels) / (sizes_all + prior_weight)
    return (labelling, centers)


def solution(mesh):
    return jax.shard_map(
        local,
        mesh=mesh,
        in_specs=(P(("gx", "gy"), None, "gz"), P()),
        out_specs=(P(None, "gx", "gy", "gz"), P()),
        check_vma=False,
    )
```

time: 41.3 us -> 36.1 us (0.87)
  Pallas kernels: 9.98 us -> 5.89 us
  local copies, waits for them, and re-layouts: 1.88 us -> 0.4 us
  waiting for transfers between devices: 10 us -> 11 us
  other arithmetic: 1.29 us -> 0.64 us
    all_to_all x1, starting transfers between devices: 7.63 us -> 11.5 us  [local(): lax.all_to_all(sent.reshape(devices, 1, ROWS * lanes), AXES, 0, 0, tiled=...]
    ppermute x1, starting transfers between devices: 4.39 us -> 0.56 us  [local(): pair = lax.ppermute(volume, SLABS, pairs)]
    pallas_call x2 -> x3, Pallas kernels: 3.97 us -> 2.23 us  [the longest x1 1.42 us: local(): pl.pallas_call(first_kernel, out_shape=[f32((devices * ROWS, lanes)), f32...]
    pallas_call x1, Pallas kernels: 3.41 us -> 2.21 us  [local(): pl.pallas_call(ahead_kernel, out_shape=[f32((labels, thick, height, depth...]
    all_to_all x1, waiting for transfers between devices: 4.27 us -> 5.47 us  [local(): lax.all_to_all(sent.reshape(devices, 1, ROWS * lanes), AXES, 0, 0, tiled=...]
    pallas_call x1, Pallas kernels: 2.59 us -> 1.46 us  [local(): pl.pallas_call(last_kernel, out_shape=[f32((devices, lanes))] + [piece] *...]
    unnamed x14 -> x4, local copies, waits for them, and re-layouts: 1.28 us -> 0.4 us
    div x1 -> x0, other arithmetic: 0.66 us -> none  [local(): base_levels = levels.astype(jnp.float32) / 255.0]
  transfers between devices with their start and end apart: 7 -> 7, of which waited for: 3 -> 3; matrix products, arithmetic and copies ran while one was open for 3% -> 2% of each run, Pallas kernels for 8% -> 6%
where the time goes in v3:
time: 36.1 us; the launch traced here: 35.9 us
  starting transfers between devices  17.2 us (48%)
  waiting for transfers between devices  11 us (30%)
  Pallas kernels  5.89 us (16%)
  between operations  0.7 us (2%)
  other arithmetic  0.64 us (2%)
  local copies, waits for them, and re-layouts  0.4 us (1%)
    all_to_all x1, starting transfers between devices, local(): lax.all_to_all(sent.reshape(devices, 1, ROWS * lanes), AXES, 0, 0, tiled=...  11.5 us
    all_to_all x1, waiting for transfers between devices, local(): lax.all_to_all(sent.reshape(devices, 1, ROWS * lanes), AXES, 0, 0, tiled=...  5.47 us
    all_to_all x1, waiting for transfers between devices, local(): lax.all_to_all(sums.reshape(devices, 1, lanes), AXES, 0, 0, tiled=True)  5.2 us
    all_to_all x1, starting transfers between devices, local(): lax.all_to_all(sums.reshape(devices, 1, lanes), AXES, 0, 0, tiled=True)  2.54 us
    pallas_call x1, Pallas kernels, local(): pl.pallas_call(ahead_kernel, out_shape=[f32((labels, thick, height, depth...  2.21 us
    ppermute x3, starting transfers between devices, local(): lax.ppermute(pieces[shift], 'gy', [(i, i ^ shift) for i in range(count)])  1.93 us
    pallas_call x1, Pallas kernels, local(): pl.pallas_call(last_kernel, out_shape=[f32((devices, lanes))] + [piece] *...  1.46 us
    pallas_call x1, Pallas kernels, local(): pl.pallas_call(first_kernel, out_shape=[f32((devices * ROWS, lanes)), f32...  1.42 us
  transfers between devices with their start and end apart: 7, of which 3 were waited for; matrix products, arithmetic and copies ran while one was open for 2% of the time, Pallas kernels for 6%

profile of v3, /device:TPU:0, one launch (start us, length us, event | category | flops | bytes accessed | tf_op | source)
XLA Modules:
  0.0 35.9 jit_solution(12275436614847831179)
XLA Ops:
  0.6 0.0 copy-start.1
  0.6 0.6 %collective-permute-start = (f32[2,64,128]{2,1,0:T(8,128)}, f32[2,64,128]{2,1,0:T(8,128)S(1)}, u32[]{:S(2)}, u32[]{:S(2)}) collective-permute-start(f32[2,64,128]{2,1,0:T(8,128)} %v_hbm.1), channel_id=1, source_target_pairs={{0,4},{4,0},{8,12},{12,8},{16,20},{20,16},{24,28},{28,24},{1,5},{5... | collective-permute-start | bytes 196616 | tf_op jit(solution)/shard_map/ppermute | solution.py:499
  1.2 0.7 %collective-permute-start.1 = (f32[2,64,128]{2,1,0:T(8,128)}, f32[2,64,128]{2,1,0:T(8,128)S(1)}, u32[]{:S(2)}, u32[]{:S(2)}) collective-permute-start(f32[2,64,128]{2,1,0:T(8,128)} %v_hbm.1), channel_id=1, source_target_pairs={{4,8},{12,16},{20,24},{8,4},{16,12},{24,20},{5,9},{13,17},{21,25},... | collective-permute-start | bytes 196616 | tf_op jit(solution)/shard_map/ppermute | solution.py:500
  1.9 0.0 copy-done.1
  1.9 0.0 copy-start
  1.9 0.1 base.1.base_ref
  2.0 0.4 %collective-permute-done.pair_ref = f32[2,64,128]{2,1,0:T(8,128)S(1)} collective-permute-done((f32[2,64,128]{2,1,0:T(8,128)}, f32[2,64,128]{2,1,0:T(8,128)S(1)}, u32[]{:S(2)}, u32[]{:S(2)}) %collective-permute-start) | collective-permute-done | bytes 65568 | tf_op jit(solution)/shard_map/ppermute | solution.py:499
  2.3 0.0 collective-permute-done.1.other_ref
  2.3 0.4 %copy-done = f32[2,64,128]{2,1,0:T(8,128)S(1)} copy-done((f32[2,64,128]{2,1,0:T(8,128)S(1)}, f32[2,64,128]{2,1,0:T(8,128)}, u32[]{:S(2)}) %copy-start) | copy-done | bytes 65560
  2.7 1.4 %first.1 = (f32[160,128]{1,0:T(8,128)}, f32[2,64,128]{2,1,0:T(8,128)S(1)}) custom-call(f32[2,64,128]{2,1,0:T(8,128)S(1)} %copy-done, f32[2,64,128]{2,1,0:T(8,128)S(1)} %collective-permute-done.pair_ref, f32[2,64,128]{2,1,0:T(8,128)S(1)} %collective-permute-done.1.other_ref, f32[4,128]{1,0:T(4,128)S(1)} %base.1.base_ref), custom_call_target="tpu_custom_call" | custom-call | tf_op jit(solution)/shard_map/first/pallas_call | solution.py:502
  4.1 11.5 %all-to-all-start = ((f32[32,1,640]{2,1,0:T(1,128)}), f32[32,1,640]{2,1,0:T(1,128)S(1)}, u32[]{:S(2)}, u32[]{:S(2)}) async-start(f32[32,1,640]{2,1,0:T(1,128)} %bitcast.1), calls=%async_computation | async-start | bytes 163840 | tf_op jit(solution)/shard_map/all_to_all | solution.py:516
  15.7 2.2 %ahead.1 = (f32[4,2,64,128]{3,2,1,0:T(8,128)S(1)}, f32[6,8,128]{2,1,0:T(8,128)S(1)}) custom-call(f32[2,64,128]{2,1,0:T(8,128)S(1)} %get-tuple-element.11.v_ref, f32[2,64,128]{2,1,0:T(8,128)S(1)} %collective-permute-done.pair_ref, f32[2,64,128]{2,1,0:T(8,128)S(1)} %collective-permute-done.1.other_ref, f32[4,128]{1,0:T(4,128)S(1)} %base.1.base_ref), custom_call_target="tpu_custom_call" | custom-call | flops 39321600 | bytes 655360 | tf_op jit(solution)/shard_map/ahead/pallas_call | solution.py:520
  17.9 5.5 %all-to-all-done = f32[32,1,640]{2,1,0:T(1,128)S(1)} async-done(((f32[32,1,640]{2,1,0:T(1,128)}), f32[32,1,640]{2,1,0:T(1,128)S(1)}, u32[]{:S(2)}, u32[]{:S(2)}) %all-to-all-start) | async-done | bytes 81952 | tf_op jit(solution)/shard_map/all_to_all | solution.py:516
  23.4 1.5 %last.1 = (f32[32,128]{1,0:T(8,128)}, f32[4,2,16,128]{3,2,1,0:T(8,128)S(1)}, f32[4,2,16,128]{3,2,1,0:T(8,128)S(1)}, f32[4,2,16,128]{3,2,1,0:T(8,128)S(1)}, f32[4,2,16,128]{3,2,1,0:T(8,128)S(1)}) custom-call(f32[2,64,128]{2,1,0:T(8,128)S(1)} %get-tuple-element.11.v_ref, f32[4,2,64,128]{3,2,1,0:T(8,128)S(1)} %get-tuple-element.12.w_ref, ...), custom_call_target="tpu_custom_call" | custom-call | tf_op jit(solution)/shard_map/last/pallas_call | solution.py:542
  24.8 2.5 %all-to-all-start.1 = ((f32[32,1,128]{2,1,0:T(1,128)}), f32[32,1,128]{2,1,0:T(1,128)S(1)}, u32[]{:S(2)}, u32[]{:S(2)}) async-start(f32[32,1,128]{2,1,0:T(1,128)} %bitcast.4), calls=%async_computation.1 | async-start | bytes 32768 | tf_op jit(solution)/shard_map/all_to_all | solution.py:552
  27.4 0.2 collective-permute-start.2
  27.6 1.6 %collective-permute-start.3 = (f32[4,2,16,128]{3,2,1,0:T(8,128)S(1)}, f32[4,2,16,128]{3,2,1,0:T(8,128)S(1)}, u32[]{:S(2)}, u32[]{:S(2)}) collective-permute-start(f32[4,2,16,128]{3,2,1,0:T(8,128)S(1)} %get-tuple-element.17), channel_id=1, source_target_pairs={{0,8},{4,12},{8,0},{12,4},{1,9},{5,13},{9,1},{13,5},{2,10},{6,14},... | collective-permute-start | bytes 196616 | tf_op jit(solution)/shard_map/ppermute | solution.py:554
  29.2 0.1 collective-permute-start.4
  29.3 5.2 %all-to-all-done.1 = f32[32,1,128]{2,1,0:T(1,128)S(1)} async-done(((f32[32,1,128]{2,1,0:T(1,128)}), f32[32,1,128]{2,1,0:T(1,128)S(1)}, u32[]{:S(2)}, u32[]{:S(2)}) %all-to-all-start.1) | async-done | bytes 16416 | tf_op jit(solution)/shard_map/all_to_all | solution.py:552
  34.5 0.1 reduce_sum.9
  34.6 0.6 %add_divide_fusion = f32[4]{0:T(128)} fusion(f32[128]{0:T(128)S(1)} %reduce_sum.9, s32[4]{0:T(128)S(1)} %copy-done.1), kind=kLoop, calls=%fused_computation | loop fusion | flops 20 | bytes 64 | tf_op jit(solution)/shard_map/div | solution.py:571
  35.1 0.0 collective-permute-done.2.refs_1_
  35.1 0.0 collective-permute-done.3.refs_2_
  35.1 0.0 collective-permute-done.4.refs_3_
  35.2 0.7 %join.1 = f32[4,8,16,128]{3,2,1,0:T(8,128)} custom-call(f32[4,2,16,128]{3,2,1,0:T(8,128)S(1)} %get-tuple-element.15.refs_0_, f32[4,2,16,128]{3,2,1,0:T(8,128)S(1)} %collective-permute-done.2.refs_1_, f32[4,2,16,128]{3,2,1,0:T(8,128)S(1)} %collective-permute-done.3.refs_2_, f32[4,2,16,128]{3,2,1,0:T(8,128)S(1)} %collective-permute-done.4.refs_3_), custom_call_target="tpu_custom_call" | custom-call | flops 65536 | bytes 524288 | tf_op jit(solution)/shard_map/join/pallas_call | solution.py:568
Async XLA Ops:
  0.6 1.2 %copy-start.1 = (s32[4]{0:T(128)S(1)}, s32[4]{0:T(128)}, u32[]{:S(2)}) copy-start(s32[4]{0:T(128)} %param.3) | copy-start | bytes 52
  0.6 1.7 %collective-permute-start = (f32[2,64,128]{2,1,0:T(8,128)}, f32[2,64,128]{2,1,0:T(8,128)S(1)}, u32[]{:S(2)}, u32[]{:S(2)}) collective-permute-start(f32[2,64,128]{2,1,0:T(8,128)} %v_hbm.1), channel_id=1, source_target_pairs={{0,4},{4,0},{8,12},{12,8},{16,20},{20,16},{24,28},{28,24},{1,5},{5... | collective-permute-start | bytes 196616 | tf_op jit(solution)/shard_map/ppermute | solution.py:499
  1.2 1.1 %collective-permute-start.1 = (f32[2,64,128]{2,1,0:T(8,128)}, f32[2,64,128]{2,1,0:T(8,128)S(1)}, u32[]{:S(2)}, u32[]{:S(2)}) collective-permute-start(f32[2,64,128]{2,1,0:T(8,128)} %v_hbm.1), channel_id=1, source_target_pairs={{4,8},{12,16},{20,24},{8,4},{16,12},{24,20},{5,9},{13,17},{21,25},... | collective-permute-start | bytes 196616 | tf_op jit(solution)/shard_map/ppermute | solution.py:500
  1.9 0.8 %copy-start = (f32[2,64,128]{2,1,0:T(8,128)S(1)}, f32[2,64,128]{2,1,0:T(8,128)}, u32[]{:S(2)}) copy-start(f32[2,64,128]{2,1,0:T(8,128)} %v_hbm.1) | copy-start | bytes 196612
  4.1 19.2 %all-to-all-start = ((f32[32,1,640]{2,1,0:T(1,128)}), f32[32,1,640]{2,1,0:T(1,128)S(1)}, u32[]{:S(2)}, u32[]{:S(2)}) async-start(f32[32,1,640]{2,1,0:T(1,128)} %bitcast.1), calls=%async_computation | async-start | bytes 163840 | tf_op jit(solution)/shard_map/all_to_all | solution.py:516
  24.8 9.7 %all-to-all-start.1 = ((f32[32,1,128]{2,1,0:T(1,128)}), f32[32,1,128]{2,1,0:T(1,128)S(1)}, u32[]{:S(2)}, u32[]{:S(2)}) async-start(f32[32,1,128]{2,1,0:T(1,128)} %bitcast.4), calls=%async_computation.1 | async-start | bytes 32768 | tf_op jit(solution)/shard_map/all_to_all | solution.py:552
  27.4 7.8 %collective-permute-start.2 = (f32[4,2,16,128]{3,2,1,0:T(8,128)S(1)}, f32[4,2,16,128]{3,2,1,0:T(8,128)S(1)}, u32[]{:S(2)}, u32[]{:S(2)}) collective-permute-start(f32[4,2,16,128]{3,2,1,0:T(8,128)S(1)} %get-tuple-element.16), channel_id=1, source_target_pairs={{0,4},{4,0},{8,12},{12,8},{1,5},{5,1},{9,13},{13,9},{2,6},{6,2},{1... | collective-permute-start | bytes 196616 | tf_op jit(solution)/shard_map/ppermute | solution.py:554
  27.6 7.6 %collective-permute-start.3 = (f32[4,2,16,128]{3,2,1,0:T(8,128)S(1)}, f32[4,2,16,128]{3,2,1,0:T(8,128)S(1)}, u32[]{:S(2)}, u32[]{:S(2)}) collective-permute-start(f32[4,2,16,128]{3,2,1,0:T(8,128)S(1)} %get-tuple-element.17), channel_id=1, source_target_pairs={{0,8},{4,12},{8,0},{12,4},{1,9},{5,13},{9,1},{13,5},{2,10},{6,14},... | collective-permute-start | bytes 196616 | tf_op jit(solution)/shard_map/ppermute | solution.py:554
  29.2 5.9 %collective-permute-start.4 = (f32[4,2,16,128]{3,2,1,0:T(8,128)S(1)}, f32[4,2,16,128]{3,2,1,0:T(8,128)S(1)}, u32[]{:S(2)}, u32[]{:S(2)}) collective-permute-start(f32[4,2,16,128]{3,2,1,0:T(8,128)S(1)} %get-tuple-element.18), channel_id=1, source_target_pairs={{0,12},{4,8},{8,4},{12,0},{1,13},{5,9},{9,5},{13,1},{2,14},{6,10},... | collective-permute-start | bytes 196616 | tf_op jit(solution)/shard_map/ppermute | solution.py:554

commit v4 on v3

--- a/solution.py
+++ b/solution.py
@@ -133,7 +133,7 @@
 
 
 CHUNK = 16
-BASE_FLOPS = 50_000_000
+COVER = 50_000_000
 
 
 def store_padded(ref, where, start, value, height):
@@ -165,60 +165,102 @@
     return (y - y_ref[where + (slice(7, 7 + height),)]) + (z - pltpu.roll(z, 1, 1))
 
 
+def pair_kernel(v_ref, pair_ref, base_ref, h_ref, e_ref, sums_ref, planes_ref, y_ref, d_ref, b_ref):
+    thick, height, depth = v_ref.shape
+    lanes = thick * height
+    labels = base_ref.shape[0]
+    terms = affine(base_of(base_ref), 0.5)
+    open_z = open_lanes(depth)
+    odd = lax.rem(slab_index(), 2)
+    sign = (1 - 2 * odd).astype(jnp.float32) * 0.0625
+    even = (1 - odd).astype(jnp.float32) * 0.0625
+    near = odd * (thick - 1)
+
+    def read(layer, rows):
+        return v_ref[layer, rows] if layer < thick else pair_ref[near, rows]
+
+    first_halves(read, range(thick + 1), height, terms, h_ref)
+    turned = jnp.transpose(v_ref[...].reshape(lanes, depth))
+    planes_ref[0:2] = turned[0:2]
+    planes_ref[2:4] = turned[depth - 2 : depth]
+    at = jnp.where(odd == 1, 2, 1)
+    following = jnp.where(odd == 1, 0, 2)
+    done = 1 - odd
+    for label in range(labels):
+        for index, (layer, after) in enumerate(((0, 1), (at, following))):
+            half = h_ref[label, layer, 0:height]
+            x = h_ref[label, after, 0:height] - half
+            y = h_ref[label, layer, 1 : height + 1] - half
+            z = (pltpu.roll(half, depth - 1, 1) - half) * open_z
+            shrink = shrink_of(x, y, z)
+            d_ref[label, index] = x * shrink
+            b_ref[label, index] = behind_yz(
+                y * shrink, z * shrink, y_ref, (label, index), height
+            )
+    sums = [None] * (2 * labels)
+    for start in range(0, height, CHUNK):
+        rows = slice(start, start + CHUNK)
+        values = v_ref[done, rows]
+        entries = []
+        for label, term in enumerate(attraction(values, terms)):
+            across = sign * (d_ref[label, 1, rows] - d_ref[label, 0, rows])
+            along = 0.0625 * b_ref[label, done, rows]
+            entries.append(h_ref[label, done, rows] + term + (across + along))
+        for label, value in enumerate(project_simplex(entries, 0.5)):
+            add_to(sums, label, value)
+            add_to(sums, labels + label, value * values)
+        values = v_ref[odd, rows]
+        for label, term in enumerate(attraction(values, terms)):
+            part = sign * d_ref[label, 0, rows] + even * b_ref[label, 0, rows]
+            e_ref[label, rows] = h_ref[label, odd, rows] + term + part
+    for index, value in enumerate(sums):
+        sums_ref[index] = value
+
+
 def first_kernel(
-    v_hbm, pair_ref, other_ref, base_ref, out_ref, v_ref, h_ref, y_ref, divergence_ref, arrived
+    v_ref, other_ref, base_ref, h_ref, e_ref, sums_in, planes_ref, out_ref, n_ref, y_ref
 ):
-    copy = pltpu.make_async_copy(v_hbm, v_ref, arrived)
-    copy.start()
     slabs = lax.axis_size(SLABS)
     blocks = lax.axis_size("gz")
     slab, block = slab_index(), lax.axis_index("gz")
-    thick, height, depth = v_hbm.shape
+    thick, height, depth = v_ref.shape
     lanes = thick * height
     devices = slabs * blocks
     labels = base_ref.shape[0]
     terms = affine(base_of(base_ref), 0.5)
     open_z = open_lanes(depth)
-    read = volume_layers(v_ref, pair_ref, other_ref, 1)
-
-    first_halves(read, (0, thick + 1), height, terms, h_ref)
-    copy.wait()
-    first_halves(read, range(1, thick + 1), height, terms, h_ref)
-    turned = jnp.transpose(v_ref[...].reshape(lanes, depth))
-    for row, plane in enumerate((0, 1, depth - 2, depth - 1)):
+    odd = lax.rem(slab, 2)
+    is_odd = odd == 1
+    left = (1 - odd) * (thick - 1)
+
+    for row in range(ROWS - 1):
         out_ref[pl.ds(row, devices, stride=ROWS), :] = jnp.broadcast_to(
-            turned[plane : plane + 1], (devices, lanes)
+            planes_ref[row : row + 1], (devices, lanes)
         )
-    inside = (slab > 0).astype(jnp.float32)
-    open_x = (slab < slabs - 1).astype(jnp.float32)
+    open_x = jnp.where(is_odd & (slab == slabs - 1), 0.0, 1.0)
+    x_scale = jnp.where(is_odd, 0.0625, jnp.where(slab > 0, -0.0625, 0.0))
+    yz_scale = jnp.where(is_odd, 0.0625, 0.0)
+    for start in range(0, height, CHUNK):
+        rows = slice(start, start + CHUNK)
+        values = other_ref[left, rows]
+        for label, half in enumerate(project_simplex(attraction(values, terms), 0.5)):
+            known = h_ref[label, odd, rows]
+            store_padded(n_ref, (label, 0), start, jnp.where(is_odd, known, half), height)
+            n_ref[label, 1, rows] = jnp.where(is_odd, half, known)
     for label in range(labels):
-        before = None
-        for layer in range(thick + 1):
-            x, y, z = gradient(h_ref, label, layer, height, depth, open_z)
-            if layer == thick:
-                x = x * open_x
-            shrink = shrink_of(x, y, z)
-            x = x * shrink
-            if layer == 0:
-                x = x * inside
-            else:
-                where = (label, layer - 1)
-                divergence_ref[where] = (x - before) + behind_yz(
-                    y * shrink, z * shrink, y_ref, where, height
-                )
-            before = x
-    sums = [None] * (2 * labels)
-    for layer in range(thick):
-        for start in range(0, height, CHUNK):
-            rows = slice(start, start + CHUNK)
-            values = v_ref[layer, rows]
-            entries = [
-                h_ref[label, layer + 1, rows] + 0.0625 * divergence_ref[label, layer, rows] + term
-                for label, term in enumerate(attraction(values, terms))
-            ]
-            for label, value in enumerate(project_simplex(entries, 0.5)):
-                add_to(sums, label, value)
-                add_to(sums, labels + label, value * values)
+        x, y, z = gradient(n_ref, label, 0, height, depth, open_z)
+        x = x * open_x
+        shrink = shrink_of(x, y, z)
+        back = behind_yz(y * shrink, z * shrink, y_ref, (label,), height)
+        n_ref[label, 1, 0:height] = x_scale * (x * shrink) + yz_scale * back
+    sums = [sums_in[index] for index in range(2 * labels)]
+    for start in range(0, height, CHUNK):
+        rows = slice(start, start + CHUNK)
+        values = v_ref[odd, rows]
+        entries = [e_ref[label, rows] + n_ref[label, 1, rows] for label in range(labels)]
+        for label, value in enumerate(project_simplex(entries, 0.5)):
+            add_to(sums, label, value)
+            add_to(sums, labels + label, value * values)
     lane = lax.broadcasted_iota(jnp.int32, (CHUNK, depth), 1)
     first = jnp.where(block > 0, 0, -1)
     last = jnp.where(block < blocks - 1, depth - 1, depth)
@@ -489,7 +531,7 @@
         in_specs=[vmem],
         out_specs=vmem,
         compiler_params=params,
-        cost_estimate=pl.CostEstimate(flops=BASE_FLOPS, bytes_accessed=0, transcendentals=0),
+        cost_estimate=pl.CostEstimate(flops=COVER, bytes_accessed=0, transcendentals=0),
         name="base",
     )(levels.reshape(1, labels))
 
@@ -499,20 +541,37 @@
     pair = lax.ppermute(volume, SLABS, pairs)
     other = lax.ppermute(volume, SLABS, across)
 
-    sent, volume = pl.pallas_call(
+    halves, entries, parts, edges = pl.pallas_call(
+        pair_kernel,
+        out_shape=[
+            f32((labels, thick + 1, height + 8, depth)),
+            f32((labels, height, depth)),
+            f32((2 * labels, CHUNK, depth)),
+            f32((4, lanes)),
+        ],
+        in_specs=[vmem] * 3,
+        out_specs=[vmem] * 4,
+        scratch_shapes=[
+            pltpu.VMEM((labels, 2, height + 8, depth), jnp.float32),
+            pltpu.VMEM((labels, 2, height, depth), jnp.float32),
+            pltpu.VMEM((labels, 2, height, depth), jnp.float32),
+        ],
+        compiler_params=params,
+        cost_estimate=pl.CostEstimate(flops=COVER, bytes_accessed=0, transcendentals=0),
+        name="pair",
+    )(volume, pair, base)
+    sent = pl.pallas_call(
         first_kernel,
-        out_shape=[f32((devices * ROWS, lanes)), f32(volume.shape)],
-        in_specs=[pl.BlockSpec(memory_space=pltpu.HBM)] + [vmem] * 3,
-        out_specs=[vmem] * 2,
+        out_shape=f32((devices * ROWS, lanes)),
+        in_specs=[vmem] * 7,
+        out_specs=vmem,
         scratch_shapes=[
-            pltpu.VMEM((labels, thick + 2, height + 8, depth), jnp.float32),
-            pltpu.VMEM((labels, thick, height + 8, depth), jnp.float32),
-            pltpu.VMEM((labels, thick, height, depth), jnp.float32),
-            pltpu.SemaphoreType.DMA,
+            pltpu.VMEM((labels, 2, height + 8, depth), jnp.float32),
+            pltpu.VMEM((labels, height + 8, depth), jnp.float32),
         ],
         compiler_params=params,
         name="first",
-    )(volume, pair, other, base)
+    )(volume, other, base, halves, entries, parts, edges)
     got = lax.all_to_all(sent.reshape(devices, 1, ROWS * lanes), AXES, 0, 0, tiled=True)
     got = got.reshape(devices * ROWS, lanes)
 

time: 36.1 us -> 35.7 us (0.989)
  starting transfers between devices: 17.2 us -> 16.5 us
    all_to_all x1, starting transfers between devices: 11.5 us -> 10.9 us  [local(): lax.all_to_all(sent.reshape(devices, 1, ROWS * lanes), AXES, 0, 0, tiled=...]
    pallas_call x1 -> x2, Pallas kernels: 1.42 us -> 1.6 us  [the longest x1 0.99 us: local(): pl.pallas_call(first_kernel, out_shape=f32((devices * ROWS, lanes)), in_s...]
  transfers between devices with their start and end apart: 7 -> 7, of which waited for: 3 -> 3; matrix products, arithmetic and copies ran while one was open for 2% -> 2% of each run, Pallas kernels for 6% -> 8%
where the time goes in v4:
time: 35.7 us; the launch traced here: 35.4 us
  starting transfers between devices  16.5 us (46%)
  waiting for transfers between devices  11 us (31%)
  Pallas kernels  6.07 us (17%)
  between operations  0.71 us (2%)
  other arithmetic  0.64 us (2%)
  local copies, waits for them, and re-layouts  0.4 us (1%)
    all_to_all x1, starting transfers between devices, local(): lax.all_to_all(sent.reshape(devices, 1, ROWS * lanes), AXES, 0, 0, tiled=...  10.9 us
    all_to_all x1, waiting for transfers between devices, local(): lax.all_to_all(sent.reshape(devices, 1, ROWS * lanes), AXES, 0, 0, tiled=...  5.47 us
    all_to_all x1, waiting for transfers between devices, local(): lax.all_to_all(sums.reshape(devices, 1, lanes), AXES, 0, 0, tiled=True)  5.2 us
    all_to_all x1, starting transfers between devices, local(): lax.all_to_all(sums.reshape(devices, 1, lanes), AXES, 0, 0, tiled=True)  2.54 us
    pallas_call x1, Pallas kernels, local(): pl.pallas_call(ahead_kernel, out_shape=[f32((labels, thick, height, depth...  2.21 us
    ppermute x3, starting transfers between devices, local(): lax.ppermute(pieces[shift], 'gy', [(i, i ^ shift) for i in range(count)])  1.93 us
    pallas_call x1, Pallas kernels, local(): pl.pallas_call(last_kernel, out_shape=[f32((devices, lanes))] + [piece] *...  1.46 us
    pallas_call x1, Pallas kernels, local(): pl.pallas_call(first_kernel, out_shape=f32((devices * ROWS, lanes)), in_s...  0.99 us
  transfers between devices with their start and end apart: 7, of which 3 were waited for; matrix products, arithmetic and copies ran while one was open for 2% of the time, Pallas kernels for 8%

profile of v4, /device:TPU:0, one launch (start us, length us, event | category | flops | bytes accessed | tf_op | source)
XLA Modules:
  0.0 35.4 jit_solution(14649780857990246772)
XLA Ops:
  0.6 0.0 copy-start.1
  0.6 0.6 %collective-permute-start = (f32[2,64,128]{2,1,0:T(8,128)}, f32[2,64,128]{2,1,0:T(8,128)S(1)}, u32[]{:S(2)}, u32[]{:S(2)}) collective-permute-start(f32[2,64,128]{2,1,0:T(8,128)} %v_ref.7), channel_id=1, source_target_pairs={{0,4},{4,0},{8,12},{12,8},{16,20},{20,16},{24,28},{28,24},{1,5},{5... | collective-permute-start | bytes 196616 | tf_op jit(solution)/shard_map/ppermute | solution.py:541
  1.2 0.7 %collective-permute-start.1 = (f32[2,64,128]{2,1,0:T(8,128)}, f32[2,64,128]{2,1,0:T(8,128)S(1)}, u32[]{:S(2)}, u32[]{:S(2)}) collective-permute-start(f32[2,64,128]{2,1,0:T(8,128)} %v_ref.7), channel_id=1, source_target_pairs={{4,8},{12,16},{20,24},{8,4},{16,12},{24,20},{5,9},{13,17},{21,25},... | collective-permute-start | bytes 196616 | tf_op jit(solution)/shard_map/ppermute | solution.py:542
  1.9 0.0 copy-done.1
  1.9 0.0 copy-start
  1.9 0.1 base.1.base_ref
  2.0 0.4 %collective-permute-done.pair_ref = f32[2,64,128]{2,1,0:T(8,128)S(1)} collective-permute-done((f32[2,64,128]{2,1,0:T(8,128)}, f32[2,64,128]{2,1,0:T(8,128)S(1)}, u32[]{:S(2)}, u32[]{:S(2)}) %collective-permute-start) | collective-permute-done | bytes 65568 | tf_op jit(solution)/shard_map/ppermute | solution.py:541
  2.3 0.4 %copy-done = f32[2,64,128]{2,1,0:T(8,128)S(1)} copy-done((f32[2,64,128]{2,1,0:T(8,128)S(1)}, f32[2,64,128]{2,1,0:T(8,128)}, u32[]{:S(2)}) %copy-start) | copy-done | bytes 65560
  2.7 0.6 %pair.1 = (f32[4,3,72,128]{3,2,1,0:T(8,128)S(1)}, f32[4,64,128]{2,1,0:T(8,128)S(1)}, f32[8,16,128]{2,1,0:T(8,128)S(1)}, f32[4,128]{1,0:T(4,128)S(1)}) custom-call(f32[2,64,128]{2,1,0:T(8,128)S(1)} %copy-done, f32[2,64,128]{2,1,0:T(8,128)S(1)} %collective-permute-done.pair_ref, f32[4,128]{1,0:T(4,128)S(1)} %base.1.base_ref), custom_call_target="tpu_custom_call" | custom-call | flops 50000000 | tf_op jit(solution)/shard_map/pair/pallas_call | solution.py:544
  3.3 0.0 collective-permute-done.1.other_ref
  3.3 1.0 %first.1 = f32[160,128]{1,0:T(8,128)} custom-call(f32[2,64,128]{2,1,0:T(8,128)S(1)} %copy-done, f32[2,64,128]{2,1,0:T(8,128)S(1)} %collective-permute-done.1.other_ref, f32[4,128]{1,0:T(4,128)S(1)} %base.1.base_ref, f32[4,3,72,128]{3,2,1,0:T(8,128)S(1)} %get-tuple-element.15.h_ref, f32[4,64,128]{2,1,0:T(8,128)S(1)} %get-tuple-element.16.e_ref, ...), custom_call_target="tpu_custom_call" | custom-call | tf_op jit(solution)/shard_map/first/pallas_call | solution.py:563
  4.3 10.9 %all-to-all-start = ((f32[32,1,640]{2,1,0:T(1,128)}), f32[32,1,640]{2,1,0:T(1,128)S(1)}, u32[]{:S(2)}, u32[]{:S(2)}) async-start(f32[32,1,640]{2,1,0:T(1,128)} %bitcast.1), calls=%async_computation | async-start | bytes 163840 | tf_op jit(solution)/shard_map/all_to_all | solution.py:575
  15.2 2.2 %ahead.1 = (f32[4,2,64,128]{3,2,1,0:T(8,128)S(1)}, f32[6,8,128]{2,1,0:T(8,128)S(1)}) custom-call(f32[2,64,128]{2,1,0:T(8,128)S(1)} %copy-done, f32[2,64,128]{2,1,0:T(8,128)S(1)} %collective-permute-done.pair_ref, f32[2,64,128]{2,1,0:T(8,128)S(1)} %collective-permute-done.1.other_ref, f32[4,128]{1,0:T(4,128)S(1)} %base.1.base_ref), custom_call_target="tpu_custom_call" | custom-call | flops 39321600 | bytes 655360 | tf_op jit(solution)/shard_map/ahead/pallas_call | solution.py:579
  17.4 5.5 %all-to-all-done = f32[32,1,640]{2,1,0:T(1,128)S(1)} async-done(((f32[32,1,640]{2,1,0:T(1,128)}), f32[32,1,640]{2,1,0:T(1,128)S(1)}, u32[]{:S(2)}, u32[]{:S(2)}) %all-to-all-start) | async-done | bytes 81952 | tf_op jit(solution)/shard_map/all_to_all | solution.py:575
  22.9 1.5 %last.1 = (f32[32,128]{1,0:T(8,128)}, f32[4,2,16,128]{3,2,1,0:T(8,128)S(1)}, f32[4,2,16,128]{3,2,1,0:T(8,128)S(1)}, f32[4,2,16,128]{3,2,1,0:T(8,128)S(1)}, f32[4,2,16,128]{3,2,1,0:T(8,128)S(1)}) custom-call(f32[2,64,128]{2,1,0:T(8,128)S(1)} %copy-done, f32[4,2,64,128]{3,2,1,0:T(8,128)S(1)} %get-tuple-element.13.w_ref, ...), custom_call_target="tpu_custom_call" | custom-call | tf_op jit(solution)/shard_map/last/pallas_call | solution.py:601
  24.4 2.5 %all-to-all-start.1 = ((f32[32,1,128]{2,1,0:T(1,128)}), f32[32,1,128]{2,1,0:T(1,128)S(1)}, u32[]{:S(2)}, u32[]{:S(2)}) async-start(f32[32,1,128]{2,1,0:T(1,128)} %bitcast.4), calls=%async_computation.1 | async-start | bytes 32768 | tf_op jit(solution)/shard_map/all_to_all | solution.py:611
  26.9 0.2 collective-permute-start.2
  27.1 1.6 %collective-permute-start.3 = (f32[4,2,16,128]{3,2,1,0:T(8,128)S(1)}, f32[4,2,16,128]{3,2,1,0:T(8,128)S(1)}, u32[]{:S(2)}, u32[]{:S(2)}) collective-permute-start(f32[4,2,16,128]{3,2,1,0:T(8,128)S(1)} %get-tuple-element.21), channel_id=1, source_target_pairs={{0,8},{4,12},{8,0},{12,4},{1,9},{5,13},{9,1},{13,5},{2,10},{6,14},... | collective-permute-start | bytes 196616 | tf_op jit(solution)/shard_map/ppermute | solution.py:613
  28.7 0.1 collective-permute-start.4
  28.8 5.2 %all-to-all-done.1 = f32[32,1,128]{2,1,0:T(1,128)S(1)} async-done(((f32[32,1,128]{2,1,0:T(1,128)}), f32[32,1,128]{2,1,0:T(1,128)S(1)}, u32[]{:S(2)}, u32[]{:S(2)}) %all-to-all-start.1) | async-done | bytes 16416 | tf_op jit(solution)/shard_map/all_to_all | solution.py:611
  34.0 0.1 reduce_sum.9
  34.1 0.6 %add_divide_fusion = f32[4]{0:T(128)} fusion(f32[128]{0:T(128)S(1)} %reduce_sum.9, s32[4]{0:T(128)S(1)} %copy-done.1), kind=kLoop, calls=%fused_computation | loop fusion | flops 20 | bytes 64 | tf_op jit(solution)/shard_map/div | solution.py:630
  34.7 0.0 collective-permute-done.2.refs_1_
  34.7 0.0 collective-permute-done.3.refs_2_
  34.7 0.0 collective-permute-done.4.refs_3_
  34.7 0.7 %join.1 = f32[4,8,16,128]{3,2,1,0:T(8,128)} custom-call(f32[4,2,16,128]{3,2,1,0:T(8,128)S(1)} %get-tuple-element.19.refs_0_, f32[4,2,16,128]{3,2,1,0:T(8,128)S(1)} %collective-permute-done.2.refs_1_, f32[4,2,16,128]{3,2,1,0:T(8,128)S(1)} %collective-permute-done.3.refs_2_, f32[4,2,16,128]{3,2,1,0:T(8,128)S(1)} %collective-permute-done.4.refs_3_), custom_call_target="tpu_custom_call" | custom-call | flops 65536 | bytes 524288 | tf_op jit(solution)/shard_map/join/pallas_call | solution.py:627
Async XLA Ops:
  0.6 1.2 %copy-start.1 = (s32[4]{0:T(128)S(1)}, s32[4]{0:T(128)}, u32[]{:S(2)}) copy-start(s32[4]{0:T(128)} %param.3) | copy-start | bytes 52
  0.6 1.7 %collective-permute-start = (f32[2,64,128]{2,1,0:T(8,128)}, f32[2,64,128]{2,1,0:T(8,128)S(1)}, u32[]{:S(2)}, u32[]{:S(2)}) collective-permute-start(f32[2,64,128]{2,1,0:T(8,128)} %v_ref.7), channel_id=1, source_target_pairs={{0,4},{4,0},{8,12},{12,8},{16,20},{20,16},{24,28},{28,24},{1,5},{5... | collective-permute-start | bytes 196616 | tf_op jit(solution)/shard_map/ppermute | solution.py:541
  1.2 2.1 %collective-permute-start.1 = (f32[2,64,128]{2,1,0:T(8,128)}, f32[2,64,128]{2,1,0:T(8,128)S(1)}, u32[]{:S(2)}, u32[]{:S(2)}) collective-permute-start(f32[2,64,128]{2,1,0:T(8,128)} %v_ref.7), channel_id=1, source_target_pairs={{4,8},{12,16},{20,24},{8,4},{16,12},{24,20},{5,9},{13,17},{21,25},... | collective-permute-start | bytes 196616 | tf_op jit(solution)/shard_map/ppermute | solution.py:542
  1.9 0.8 %copy-start = (f32[2,64,128]{2,1,0:T(8,128)S(1)}, f32[2,64,128]{2,1,0:T(8,128)}, u32[]{:S(2)}) copy-start(f32[2,64,128]{2,1,0:T(8,128)} %v_ref.7) | copy-start | bytes 196612
  4.3 18.6 %all-to-all-start = ((f32[32,1,640]{2,1,0:T(1,128)}), f32[32,1,640]{2,1,0:T(1,128)S(1)}, u32[]{:S(2)}, u32[]{:S(2)}) async-start(f32[32,1,640]{2,1,0:T(1,128)} %bitcast.1), calls=%async_computation | async-start | bytes 163840 | tf_op jit(solution)/shard_map/all_to_all | solution.py:575
  24.4 9.7 %all-to-all-start.1 = ((f32[32,1,128]{2,1,0:T(1,128)}), f32[32,1,128]{2,1,0:T(1,128)S(1)}, u32[]{:S(2)}, u32[]{:S(2)}) async-start(f32[32,1,128]{2,1,0:T(1,128)} %bitcast.4), calls=%async_computation.1 | async-start | bytes 32768 | tf_op jit(solution)/shard_map/all_to_all | solution.py:611
  26.9 7.8 %collective-permute-start.2 = (f32[4,2,16,128]{3,2,1,0:T(8,128)S(1)}, f32[4,2,16,128]{3,2,1,0:T(8,128)S(1)}, u32[]{:S(2)}, u32[]{:S(2)}) collective-permute-start(f32[4,2,16,128]{3,2,1,0:T(8,128)S(1)} %get-tuple-element.20), channel_id=1, source_target_pairs={{0,4},{4,0},{8,12},{12,8},{1,5},{5,1},{9,13},{13,9},{2,6},{6,2},{1... | collective-permute-start | bytes 196616 | tf_op jit(solution)/shard_map/ppermute | solution.py:613
  27.1 7.6 %collective-permute-start.3 = (f32[4,2,16,128]{3,2,1,0:T(8,128)S(1)}, f32[4,2,16,128]{3,2,1,0:T(8,128)S(1)}, u32[]{:S(2)}, u32[]{:S(2)}) collective-permute-start(f32[4,2,16,128]{3,2,1,0:T(8,128)S(1)} %get-tuple-element.21), channel_id=1, source_target_pairs={{0,8},{4,12},{8,0},{12,4},{1,9},{5,13},{9,1},{13,5},{2,10},{6,14},... | collective-permute-start | bytes 196616 | tf_op jit(solution)/shard_map/ppermute | solution.py:613
  28.7 5.9 %collective-permute-start.4 = (f32[4,2,16,128]{3,2,1,0:T(8,128)S(1)}, f32[4,2,16,128]{3,2,1,0:T(8,128)S(1)}, u32[]{:S(2)}, u32[]{:S(2)}) collective-permute-start(f32[4,2,16,128]{3,2,1,0:T(8,128)S(1)} %get-tuple-element.22), channel_id=1, source_target_pairs={{0,12},{4,8},{8,4},{12,0},{1,13},{5,9},{9,5},{13,1},{2,14},{6,10},... | collective-permute-start | bytes 196616 | tf_op jit(solution)/shard_map/ppermute | solution.py:613
